TPU v7x, 32 devices: a whole 2x2x4 slice. The times are simulated.
32 devices in a mesh: grp: 4 (over y, x), seq: 2 (over core), mdl: 4 (over z).
Axes of the slice: x: 2, y: 2, z: 4, core: 2. Of those that a mesh axis runs over, the one named last changes fastest.
Arguments:
- layer_input: bfloat16 [1024, 8192], P('seq', 'grp'), may hold values from -64 to 64
- attn_weight: bfloat16 [8192, 8, 1280], P(('grp', 'seq'), 'mdl'), may hold values from -0.0625 to 0.0625
- rate_weight: bfloat16 [8192, 64], P('grp', 'mdl'), may hold values from -0.15625 to 0.15625
- rate_bias: float32 [64], P(('mdl', 'grp')), may hold values from -8 to -3
- decay_rate: float32 [64], P(('mdl', 'grp')), may hold values from 1e-05 to 0.1
- skip_gain: float32 [64], P(('mdl', 'grp')), may hold values from 0.5 to 1.5
Outputs:
- teacher_heads: bfloat16 [1024, 8192], P('seq', ('mdl', 'grp'))
- student_heads: bfloat16 [1024, 8192], P('seq', ('mdl', 'grp'))
All inputs are finite; a program needn't handle non-finite values.
Results may differ from a plain program's by a relative error of at most 0.03.
Values may be sent and summed in bfloat16 or wider, within the bound.
No kernel may reach another device: no remote copies, remote signals or barrier semaphores. Data moves between devices by JAX's collectives and lax.ppermute only.
A program may use at most 192 MiB of HBM per device.

v0:
```python
import functools
import math

import jax
import jax.numpy as jnp
from jax import lax
from jax.experimental import pallas as pl
from jax.experimental.pallas import tpu as pltpu
from jax.sharding import PartitionSpec as P


HEADS = 64
KV_HEADS = 8
HEAD_DIM = 128
STRETCH = 256


ROPE_BASE = 500000.0
FAR_BELOW = -1e30


def rope_angles(positions):
    half = HEAD_DIM // 2
    freq = ROPE_BASE ** (-2.0 * jnp.arange(half, dtype=jnp.float32) / HEAD_DIM)
    angle = positions.astype(jnp.float32)[:, None] * freq[None, :]
    return (jnp.cos(angle), jnp.sin(angle))


def rotate(vectors, cosine, sine):
    half = vectors.shape[-1] // 2
    first = vectors[..., :half]
    second = vectors[..., half:]
    cosine = cosine[:, None, :]
    sine = sine[:, None, :]
    return jnp.concatenate(
        [first * cosine - second * sine, second * cosine + first * sine], axis=-1
    )


def state_product(cterm, state):
    high = state.astype(jnp.bfloat16)
    low = (state - high.astype(jnp.float32)).astype(jnp.bfloat16)
    upper = jnp.einsum("thn,hnp->thp", cterm, high, preferred_element_type=jnp.float32)
    return upper + jnp.einsum("thn,hnp->thp", cterm, low, preferred_element_type=jnp.float32)


def key_absorber(queries, own_first, scale, carry, piece):
    top, total, accum = carry
    keys, values = piece
    scores = jnp.einsum("thd,nd->thn", queries, keys, preferred_element_type=jnp.float32) * scale
    query_pos = own_first + jnp.arange(queries.shape[0], dtype=jnp.int32)
    key_pos = jnp.arange(keys.shape[0], dtype=jnp.int32)
    causal = (key_pos[None, :] <= query_pos[:, None])[:, None, :]
    masked = jnp.where(causal, scores, FAR_BELOW)
    new_top = jnp.maximum(top, jnp.max(masked, axis=2))
    weights = jnp.where(causal, jnp.exp(masked - new_top[:, :, None]), 0.0)
    total = jnp.sum(weights, axis=2)
    accum = jnp.einsum(
        "thn,nd->thd", weights.astype(jnp.bfloat16), values, preferred_element_type=jnp.float32
    )
    return (new_top, total, accum)


def body(layer_input, attn_weight, rate_weight, rate_bias, decay_rate, skip_gain):
    tok = layer_input.shape[0]
    kv_local = attn_weight.shape[1]
    heads_local = rate_bias.shape[0]
    group = HEADS // KV_HEADS
    scale = HEAD_DIM ** (-0.5)
    merged = jnp.einsum(
        "td,dkc->tkc",
        layer_input,
        lax.all_gather(attn_weight, "seq", axis=0, tiled=True),
        preferred_element_type=jnp.float32,
    )
    rate_part = jnp.dot(layer_input, rate_weight, preferred_element_type=jnp.float32)
    grp_index = lax.axis_index("grp")
    summed, rate_whole = (
        lax.psum(merged.astype(jnp.bfloat16), "grp").astype(jnp.float32),
        lax.psum(rate_part.astype(jnp.bfloat16), "grp").astype(jnp.float32),
    )
    query_whole = summed[:, :, : group * HEAD_DIM].reshape(tok, kv_local * group * HEAD_DIM)
    query_flat = lax.dynamic_slice_in_dim(
        query_whole, grp_index * heads_local * HEAD_DIM, heads_local * HEAD_DIM, 1
    )
    raw = lax.dynamic_slice_in_dim(rate_whole, grp_index * heads_local, heads_local, 1)
    pairs = summed[:, :, group * HEAD_DIM :]
    kv_index = grp_index * heads_local // group
    pair = lax.dynamic_index_in_dim(pairs, kv_index, 1, keepdims=False)
    keys = pair[:, :HEAD_DIM]
    values = pair[:, HEAD_DIM:].astype(jnp.bfloat16)
    query = query_flat.reshape(tok, heads_local, HEAD_DIM)
    own_first = lax.axis_index("seq") * tok
    cosine, sine = rope_angles(own_first + jnp.arange(tok, dtype=jnp.int32))
    rot_query = rotate(query, cosine, sine).astype(jnp.bfloat16)
    rot_keys = rotate(keys[:, None, :], cosine, sine)[:, 0].astype(jnp.bfloat16)
    start_carry = (
        jnp.full((tok, heads_local), FAR_BELOW, jnp.float32),
        jnp.zeros((tok, heads_local), jnp.float32),
        jnp.zeros((tok, heads_local, HEAD_DIM), jnp.float32),
    )
    _, total, accum = key_absorber(
        rot_query,
        own_first,
        scale,
        start_carry,
        (
            lax.all_gather(rot_keys, "seq", axis=0, tiled=True),
            lax.all_gather(values, "seq", axis=0, tiled=True),
        ),
    )
    teacher = (accum / total[:, :, None]).astype(jnp.bfloat16).reshape(tok, heads_local * HEAD_DIM)
    step = jax.nn.softplus(raw + rate_bias[None, :])
    log_decay = -decay_rate[None, :] * step
    c_all = query.astype(jnp.bfloat16)
    b_all = keys.astype(jnp.bfloat16)
    causal = (
        jnp.arange(STRETCH, dtype=jnp.int32)[:, None]
        >= jnp.arange(STRETCH, dtype=jnp.int32)[None, :]
    )[None]
    state = jnp.zeros((heads_local, HEAD_DIM, HEAD_DIM), jnp.float32)
    before = jnp.zeros((heads_local,), jnp.float32)
    partials = []
    offsets = []
    for index in range(tok // STRETCH):
        first = index * STRETCH
        cpart = c_all[first : first + STRETCH]
        bpart = b_all[first : first + STRETCH]
        xpart = values[first : first + STRETCH]
        decay = log_decay[first : first + STRETCH]
        rate = step[first : first + STRETCH]
        cum = jnp.cumsum(decay, axis=0)
        gram = jnp.einsum("thn,sn->hts", cpart, bpart, preferred_element_type=jnp.float32) * scale
        diff = cum.T[:, :, None] - cum.T[:, None, :]
        mix = jnp.where(
            causal, jnp.exp(jnp.where(causal, diff, -10000.0)) * rate.T[:, None, :] * gram, 0.0
        ).astype(jnp.bfloat16)
        intra = jnp.einsum("hts,sp->thp", mix, xpart, preferred_element_type=jnp.float32)
        carried = state_product(cpart, state) * scale * jnp.exp(cum)[:, :, None]
        weighted = (
            (jnp.exp(cum[-1][None, :] - cum) * rate)[:, :, None]
            * bpart.astype(jnp.float32)[:, None, :]
        ).astype(jnp.bfloat16)
        contribution = jnp.einsum(
            "shn,sp->hnp", weighted, xpart, preferred_element_type=jnp.float32
        )
        state = jnp.exp(cum[-1])[:, None, None] * state + contribution
        partials.append(intra + carried)
        offsets.append(cum + before[None, :])
        before = before + cum[-1]
    totals, states = (
        lax.all_gather(before[None, :].astype(jnp.bfloat16), "seq", axis=0, tiled=True).astype(
            jnp.float32
        ),
        lax.all_gather(state[None].astype(jnp.bfloat16), "seq", axis=0, tiled=True).astype(
            jnp.float32
        ),
    )
    position = lax.axis_index("seq")
    order = jnp.arange(totals.shape[0], dtype=jnp.int32)
    between = ((order[:, None] < order[None, :]) & (order[None, :] < position)).astype(jnp.float32)
    span = jnp.dot(between, totals, precision=lax.Precision.HIGHEST)
    reach_back = jnp.where(order[:, None] < position, jnp.exp(span), 0.0)
    incoming = jnp.einsum("dh,dhnp->hnp", reach_back, states, precision=lax.Precision.HIGHEST)
    inside = jnp.concatenate(partials, axis=0)
    reach = jnp.exp(jnp.concatenate(offsets, axis=0))
    arriving = state_product(c_all, incoming) * scale * reach[:, :, None]
    skipped = skip_gain[None, :, None] * values.astype(jnp.float32)[:, None, :]
    student = (
        (inside + arriving + skipped).astype(jnp.bfloat16).reshape(tok, heads_local * HEAD_DIM)
    )
    return (teacher, student)


LANES = 128
EXTRA = 16
GRANTS = tuple(mib * 1024 * 1024 for mib in (6, 12, 16, 24))
F32 = jnp.float32
BF16 = jnp.bfloat16
LAST = (((1,), (1,)), ((), ()))


def cost(flops, moved):
    return pl.CostEstimate(flops=flops, bytes_accessed=moved, transcendentals=0)


def place_of():
    grp = lax.axis_index("grp")
    return grp // 2, grp % 2, lax.axis_index("seq")


def gathered(w_ref, blocks):
    return jnp.concatenate(
        [w_ref[kv, :, pl.ds(pl.multiple_of(col * LANES, LANES), LANES)] for kv, col in blocks], axis=1
    )


def own_columns(x_ref, rows):
    first = pl.multiple_of(lax.axis_index("seq") * rows, LANES)
    return x_ref[:, pl.ds(first, rows)]


def project_kernel(places, order, x_ref, w_ref, out_ref):
    high, low, _ = place_of()
    weights = gathered(w_ref, places(high, low))
    out_ref[...] = jnp.dot(
        own_columns(x_ref, w_ref.shape[1]), weights, preferred_element_type=F32
    ).astype(BF16)


def project_add_kernel(places, order, x_ref, w_ref, r_ref, send_ref, keep_ref):
    high, low, _ = place_of()
    blocks = places(high, low)
    tok, half = keep_ref.shape
    tokens = own_columns(x_ref, w_ref.shape[1])
    first = jnp.dot(tokens, gathered(w_ref, blocks[:2]), preferred_element_type=F32)
    send_ref[:tok, :] = (first + r_ref[:, :half].astype(F32)).astype(BF16)
    second = jnp.dot(tokens, gathered(w_ref, blocks[2:]), preferred_element_type=F32)
    keep_ref[...] = second + r_ref[:, half:].astype(F32)


def folded(rates):
    parts = rates.shape[1] // LANES
    return jnp.concatenate([rates[:, i * LANES : (i + 1) * LANES] for i in range(parts)], axis=0)


def unfolded(rows, count):
    parts = rows.shape[0] // count
    return jnp.concatenate([rows[i * count : (i + 1) * count] for i in range(parts)], axis=1)


def project_pair_kernel(places, order, raw_ref, x_ref, w_ref, r_ref, keys_ref, values_ref, keep_ref):
    high, low, _ = place_of()
    blocks = places(high, low)
    tok, half = keep_ref.shape
    tokens = own_columns(x_ref, w_ref.shape[1])
    first = jnp.dot(tokens, gathered(w_ref, blocks[:2]), preferred_element_type=F32)
    first = (first + r_ref[:, :half].astype(F32)).astype(BF16)
    keys_ref[:tok, :] = first[:, :LANES]
    values_ref[...] = first[:, LANES:]
    second = jnp.dot(tokens, gathered(w_ref, blocks[2:]), preferred_element_type=F32)
    keep_ref[...] = second + r_ref[:, half:].astype(F32)
    away = EXTRA // 2
    rates = jnp.where(high == 0, raw_ref[away:, :], raw_ref[:away, :])
    keys_ref[tok:, :] = folded(rates).astype(BF16)


def own_rates(raw_ref, u_ref):
    tok = raw_ref.shape[1]
    own = EXTRA // 2
    rates = jnp.where(place_of()[0] == 0, raw_ref[:own, :], raw_ref[own:, :])
    return rates + unfolded(u_ref[tok:, :].astype(F32), own)


def keys_middle_kernel(order, raw_ref, keep_ref, u_ref, send_ref):
    tok = keep_ref.shape[0]
    send_ref[:tok, :] = (keep_ref[:, :LANES] + u_ref[:tok, :].astype(F32)).astype(BF16)
    send_ref[tok:, :] = folded(own_rates(raw_ref, u_ref)).astype(BF16)


def values_middle_kernel(order, keep_ref, u_ref, send_ref):
    send_ref[...] = (keep_ref[:, LANES:] + u_ref[...].astype(F32)).astype(BF16)


def middle_kernel(order, keep_ref, u_ref, send_ref):
    send_ref[...] = (keep_ref[:, :LANES] + u_ref[:, :LANES].astype(F32)).astype(BF16)


def prepare_kernel(order, x_ref, rates_ref, raw_ref, cos_ref, sin_ref):
    raw_ref[...] = lax.dot_general(
        rates_ref[...], x_ref[...], LAST, preferred_element_type=F32
    )
    tok, wide = cos_ref.shape
    half = wide // 2
    fine = EXTRA
    lane = lax.broadcasted_iota(jnp.int32, (1, wide), 1)
    slot = jnp.where(lane < half, lane, lane - half).astype(F32)
    freq = jnp.exp(slot * (-2.0 / wide * math.log(ROPE_BASE)))
    start = lax.axis_index("seq") * tok
    coarse = lax.broadcasted_iota(jnp.int32, (tok // fine, wide), 0) * fine + start
    coarse = coarse.astype(F32) * freq
    small = lax.broadcasted_iota(jnp.int32, (fine, wide), 0).astype(F32) * freq
    cos_big, sin_big = jnp.cos(coarse), jnp.sin(coarse)
    cos_small, sin_small = jnp.cos(small), jnp.sin(small)
    sign = jnp.where(lane < half, -1.0, 1.0)
    for at in range(tok // fine):
        c, d = cos_big[at : at + 1, :], sin_big[at : at + 1, :]
        span = slice(at * fine, (at + 1) * fine)
        cos_ref[span, :] = c * cos_small - d * sin_small
        sin_ref[span, :] = (d * cos_small + c * sin_small) * sign


VMEM = pl.BlockSpec(memory_space=pltpu.VMEM)
SMEM = pl.BlockSpec(memory_space=pltpu.SMEM)
ANY = pl.BlockSpec(memory_space=pl.ANY)


def call(kernel, order, args, shapes, flops, in_specs=None, **rest):
    return pl.pallas_call(
        kernel,
        in_specs=[ANY] + (in_specs or [VMEM] * len(args)),
        out_specs=rest.pop("out_specs", [VMEM] * len(shapes)),
        out_shape=[jax.ShapeDtypeStruct(s, d) for s, d in shapes],
        compiler_params=pltpu.CompilerParams(vmem_limit_bytes=rest.pop("grant", GRANTS[1])),
        cost_estimate=cost(flops, 3 * 10**6),
        **rest,
    )(order, *args)


def project(order, x, weights, places):
    tok, rows = x.shape[0], weights.shape[1]
    wide = 4 * LANES
    return call(
        functools.partial(project_kernel, places), order, [x, weights],
        [((tok, wide), BF16)], 2 * tok * rows * wide,
    )


def project_add(order, x, weights, places, received, raw):
    tok, rows = x.shape[0], weights.shape[1]
    wide = 4 * LANES
    args, kernel = [x, weights, received], project_add_kernel
    kept = ((tok, wide // 2), F32)
    if raw is None:
        shapes = [((tok, wide // 2), BF16), kept]
    else:
        args, kernel = [raw] + args, project_pair_kernel
        tall = tok + EXTRA // 2 * tok // LANES
        shapes = [((tall, LANES), BF16), ((tok, LANES), BF16), kept]
    return call(functools.partial(kernel, places), order, args, shapes, 2 * tok * rows * wide)


def turn(vectors, cosine, sine):
    return vectors * cosine + pltpu.roll(vectors, HEAD_DIM // 2, 1) * sine


def split_sum(rows, mask):
    high = rows.astype(BF16)
    rest = rows - high.astype(F32)
    middle = rest.astype(BF16)
    low = (rest - middle.astype(F32)).astype(BF16)
    count = rows.shape[0]
    parts = jnp.concatenate([high.astype(F32), middle.astype(F32), low.astype(F32)], axis=0)
    sums = lax.dot_general(parts.astype(BF16), mask, LAST, preferred_element_type=F32)
    return sums[:count] + (sums[count : 2 * count] + sums[2 * count :])


def upright(row):
    count = row.shape[1]
    down = lax.broadcasted_iota(jnp.int32, (count, count), 0)
    along = lax.broadcasted_iota(jnp.int32, (count, count), 1)
    return jnp.sum(jnp.where(down == along, row, 0.0), axis=1, keepdims=True)


def context_kernel(
    stretch, order, raw_ref, keep_ref, u_ref, u_values_ref, z_ref, z_values_ref, cos_ref, sin_ref,
    bias_ref, rate_ref,
    carry_ref, bterm_ref, across_ref, down_ref, step_ref, first_ref,
):
    tok = keep_ref.shape[0]
    heads = bias_ref.shape[1]
    spans = tok // stretch
    keys = keep_ref[:, :LANES] + u_ref[:tok, :].astype(F32) + z_ref[:tok, :].astype(F32)
    values = keep_ref[:, LANES:] + u_values_ref[...].astype(F32) + z_values_ref[...].astype(F32)
    values = values.astype(BF16)
    bterm = keys.astype(BF16)
    carry_ref[:tok, :HEAD_DIM] = turn(keys, cos_ref[...], sin_ref[...]).astype(BF16)
    carry_ref[:tok, HEAD_DIM:] = values
    bterm_ref[...] = bterm
    both = own_rates(raw_ref, u_ref) + unfolded(z_ref[tok:, :].astype(F32), EXTRA // 2)
    raw = jnp.where(place_of()[1] == 0, both[:heads], both[heads:])
    bias, rate = upright(bias_ref[...]), upright(rate_ref[...])
    step = jax.nn.softplus(raw + bias)
    decay = -rate * step
    rows = lax.broadcasted_iota(jnp.int32, (stretch, stretch), 0)
    cols = lax.broadcasted_iota(jnp.int32, (stretch, stretch), 1)
    below = (cols <= rows).astype(F32).astype(BF16)
    fold = lambda a: jnp.concatenate([a[:, i * stretch : (i + 1) * stretch] for i in range(spans)], axis=0)
    across = split_sum(fold(decay), below)
    steps = fold(step)
    tails = jnp.exp(across[:, stretch - 1 :] - across) * steps
    across_ref[...] = across
    step_ref[...] = steps
    count = heads * spans
    filler = jnp.zeros((LANES - 2 * count, stretch), F32)
    down = jnp.transpose(jnp.concatenate([across, tails, filler], axis=0))
    down_ref[...] = down
    states = [None] * heads
    for index in range(spans):
        span = slice(index * stretch, (index + 1) * stretch)
        part = bterm[span].astype(F32)
        weighted = jnp.concatenate(
            [
                (part * down[:, count + index * heads + h : count + index * heads + h + 1]).astype(BF16)
                for h in range(heads)
            ],
            axis=1,
        )
        fresh = lax.dot_general(
            weighted, values[span], (((0,), (0,)), ((), ())), preferred_element_type=F32
        )
        for h in range(heads):
            new = fresh[h * HEAD_DIM : (h + 1) * HEAD_DIM]
            if index > 0:
                at = index * heads + h
                new = new + jnp.exp(across[at : at + 1, stretch - 1 :]) * states[h]
            else:
                first_ref[h] = new
            states[h] = new
    for h in range(heads):
        row, col = tok + (h // 2) * HEAD_DIM, (h % 2) * HEAD_DIM
        carry_ref[row : row + HEAD_DIM, col : col + HEAD_DIM] = states[h].astype(BF16)


def head_kernel(
    stretch, head, order, keep_ref, u_ref, z_ref, cos_ref, sin_ref, carry_ref, bterm_ref, came_ref,
    across_ref, down_ref, step_ref, first_ref, skip_ref, *rest,
):
    if len(rest) == 2:
        teacher_ref, student_ref = rest
    else:
        teacher_out, student_out, teacher_ref, student_ref, sems = rest[-5:]
        before, copies = rest[:-5], []
        for at, held in enumerate(before):
            number, kind = at // 2, at % 2
            number = number + (number >= head)
            out = (teacher_out, student_out)[kind]
            place = slice(number * HEAD_DIM, (number + 1) * HEAD_DIM)
            copies.append(pltpu.make_async_copy(held, out.at[:, place], sems.at[at]))
            copies[-1].start()
    tok = bterm_ref.shape[0]
    heads = first_ref.shape[0]
    scale = HEAD_DIM ** (-0.5)
    power = scale * 1.4426950408889634
    later = (lax.axis_index("seq") > 0).astype(F32)
    blocked = (1.0 - later) * FAR_BELOW
    rows = lax.broadcasted_iota(jnp.int32, (stretch, stretch), 0)
    cols = lax.broadcasted_iota(jnp.int32, (stretch, stretch), 1)
    causal = cols <= rows
    ones = jnp.ones((tok, HEAD_DIM), BF16)
    own_keys = carry_ref[:tok, :HEAD_DIM]
    prev_keys = came_ref[:tok, :HEAD_DIM]
    own_values = jnp.concatenate([carry_ref[:tok, HEAD_DIM:], ones], axis=1)
    prev_values = jnp.concatenate([came_ref[:tok, HEAD_DIM:], ones], axis=1)
    query = keep_ref[:, LANES:] + u_ref[:, LANES:].astype(F32) + z_ref[...].astype(F32)
    turned = turn(query, cos_ref[...], sin_ref[...]).astype(BF16)
    cterm = query.astype(BF16)
    row, col = tok + (head // 2) * HEAD_DIM, (head % 2) * HEAD_DIM
    state = came_ref[row : row + HEAD_DIM, col : col + HEAD_DIM].astype(F32) * later
    skip = skip_ref[:, head : head + 1]
    for index in range(tok // stretch):
        span = slice(index * stretch, (index + 1) * stretch)
        reach = (index + 1) * stretch
        queries = turned[span]
        far = lax.dot_general(queries, prev_keys, LAST, preferred_element_type=F32) + blocked
        near = lax.dot_general(queries, own_keys[:reach], LAST, preferred_element_type=F32)
        diagonal = jnp.where(causal, near[:, index * stretch :], FAR_BELOW)
        if index > 0:
            near = jnp.concatenate([near[:, : index * stretch], diagonal], axis=1)
        else:
            near = diagonal
        top = jnp.maximum(
            jnp.max(far, axis=1, keepdims=True), jnp.max(near, axis=1, keepdims=True)
        )
        far = jnp.exp2((far - top) * power).astype(BF16)
        near = jnp.exp2((near - top) * power).astype(BF16)
        mixed = jnp.dot(far, prev_values, preferred_element_type=F32) + jnp.dot(
            near, own_values[:reach], preferred_element_type=F32
        )
        teacher_ref[span, :] = (mixed[:, :HEAD_DIM] / mixed[:, HEAD_DIM:]).astype(BF16)
        values = carry_ref[span, HEAD_DIM:]
        which = index * heads + head
        down = down_ref[:, which : which + 1]
        across = across_ref[which : which + 1, :]
        gram = lax.dot_general(
            cterm[span], bterm_ref[span, :], LAST, preferred_element_type=F32
        ) * (step_ref[which : which + 1, :] * scale)
        mix = jnp.where(causal, jnp.exp(jnp.where(causal, down - across, -1e4)) * gram, 0.0)
        inner = jnp.dot(mix.astype(BF16), values, preferred_element_type=F32)
        high = state.astype(BF16)
        low = (state - high.astype(F32)).astype(BF16)
        carried = jnp.dot(
            cterm[span], jnp.concatenate([high, low], axis=1), preferred_element_type=F32
        )
        carried = (carried[:, :HEAD_DIM] + carried[:, HEAD_DIM:]) * (jnp.exp(down) * scale)
        student_ref[span, :] = (inner + carried + skip * values.astype(F32)).astype(BF16)
        if index == 0:
            state = jnp.exp(across[:, stretch - 1 :]) * state + first_ref[head]
    if len(rest) > 2:
        place = slice(head * HEAD_DIM, (head + 1) * HEAD_DIM)
        for kind, (held, out) in enumerate(((teacher_ref, teacher_out), (student_ref, student_out))):
            copies.append(
                pltpu.make_async_copy(held, out.at[:, place], sems.at[len(before) + kind])
            )
            copies[-1].start()
        for copy in copies:
            copy.wait()


def head_call(order, head, piece, shared, total, before):
    tok = piece[0].shape[0]
    args = list(piece) + list(shared)
    kernel = functools.partial(head_kernel, STRETCH, head)
    if before is None:
        return call(kernel, order, args, [((tok, HEAD_DIM), BF16)] * 2, 10**9, grant=GRANTS[2])
    args += before
    held = pltpu.VMEM((tok, HEAD_DIM), BF16)
    return call(
        kernel, order, args, [((tok, total), BF16)] * 2, 10**9, out_specs=[ANY] * 2, grant=GRANTS[2],
        scratch_shapes=[held, held, pltpu.SemaphoreType.DMA((len(before) + 2,))],
    )


def pair_body(*args):
    return pair_steps(*args)


def pair_steps(layer_input, attn_weight, rate_weight, rate_bias, decay_rate, skip_gain):
    tok, _ = layer_input.shape
    heads = rate_bias.shape[0]
    group = HEADS // KV_HEADS
    ids = skip_gain[:1]
    count = lax.axis_size("grp")
    swap_high = [(g, g ^ 2) for g in range(count)]
    swap_low = [(g, g ^ 1) for g in range(count)]
    over_high = lambda a: lax.ppermute(a, "grp", swap_high)
    over_low = lambda a: lax.ppermute(a, "grp", swap_low)
    over_seq = lambda a: lax.ppermute(a, "seq", [(0, 1), (1, 0)])

    other = over_seq(layer_input)
    weights_all = jnp.transpose(attn_weight, (1, 0, 2))
    shapes = [((EXTRA, tok), F32), ((tok, HEAD_DIM), F32), ((tok, HEAD_DIM), F32)]

    def pair_places(h, l):
        return [(1 - h, group), (1 - h, group + 1), (h, group), (h, group + 1)]

    def high_places(j):
        return lambda h, l: [
            (1 - h, (1 - l) * heads + j), (1 - h, l * heads + j),
            (h, (1 - l) * heads + j), (h, l * heads + j),
        ]

    def low_places(j):
        return lambda h, l: [
            (1 - h, (1 - l) * heads + j), (h, (1 - l) * heads + j),
            (1 - h, l * heads + j), (h, l * heads + j),
        ]

    ahead = [(ids, weights_all)]

    def queued(make):
        ready, _ = lax.optimization_barrier((ids, ahead[0]))
        outs = make(ready)
        ahead[0] = outs[0]
        return outs

    def prepare():
        return queued(
            lambda ready: call(prepare_kernel, ready, [layer_input, rate_weight.T], shapes, 10**9)
        )

    raw, cosine, sine = prepare()
    other, weights_all, raw = lax.optimization_barrier((other, weights_all, raw))
    plan = [(None, weights_all, pair_places, over_high, over_low)]
    for pair in range(heads // 2):
        plan.append((2 * pair + 1, weights_all, low_places(2 * pair + 1), over_low, over_high))
        plan.append((2 * pair, weights_all, high_places(2 * pair), over_high, over_low))
    crossed, parts, arrived, pieces, kept = {}, {}, {}, {}, {}

    def cross(at):
        _, weights, places, _, _ = plan[at]
        out = queued(lambda ready: project(ready, other, weights, places))[0]
        crossed[at] = over_seq(out)

    def mine(at):
        j, weights, places, first, _ = plan[at]
        *sends, kept[at] = queued(
            lambda ready: project_add(
                ready, layer_input, weights, places, crossed[at], raw if j is None else None
            )
        )
        if j is None:
            for name, send in zip("kv", sends):
                parts[name] = first(send)
        else:
            parts[at] = first(sends[0])

    def middle(at):
        j, _, _, _, second = plan[0 if at in ("k", "v") else at]
        keep, u = kept[0 if at in ("k", "v") else at], parts[at]
        args, shapes, kernel = [keep, u], [((tok, LANES), BF16)], middle_kernel
        if at == "k":
            args, shapes, kernel = [raw, keep, u], [(u.shape, BF16)], keys_middle_kernel
        if at == "v":
            kernel = values_middle_kernel
        send = queued(lambda ready: call(kernel, ready, args, shapes, 10**7))[0]
        arrived[at] = second(send)
        if j is not None:
            pieces[j] = (keep, u, arrived[at])

    def context():
        args = [
            raw, kept[0], parts["k"], parts["v"], arrived["k"], arrived["v"], cosine, sine, rate_bias[None, :], decay_rate[None, :],
        ]
        spans = tok // STRETCH
        shapes = [
            ((tok + heads // 2 * HEAD_DIM, 2 * HEAD_DIM), BF16), ((tok, HEAD_DIM), BF16),
            ((heads * spans, STRETCH), F32), ((STRETCH, LANES), F32), ((heads * spans, STRETCH), F32),
            ((heads, HEAD_DIM, HEAD_DIM), F32),
        ]
        carry, *rest = queued(
            lambda ready: call(
                functools.partial(context_kernel, STRETCH), ready, args, shapes, 10**9,
                grant=GRANTS[2],
            )
        )
        came = over_seq(carry)
        bterm, across, down, step, first_state = rest
        return (
            cosine, sine, carry, bterm, came, across, down, step, first_state, skip_gain[None, :],
        )

    def tail(j, shared, before):
        return queued(
            lambda ready: head_call(ready, j, pieces[j], shared, heads * HEAD_DIM, before)
        )

    cross(0)
    cross(1)
    cross(2)
    mine(0)
    mine(1)
    mine(2)
    cross(3)
    middle("k")
    cross(4)
    middle("v")
    mine(3)
    middle(1)
    mine(4)
    middle(2)
    shared = context()
    done = {1: tail(1, shared, None)}
    middle(3)
    middle(4)
    for j in (0, 3):
        done[j] = tail(j, shared, None)
    outs = tail(2, shared, [part for j in sorted(done) for part in done[j]])
    return outs[0], outs[1]


def solution(mesh):
    placed = (
        P("seq", "grp"),
        P(("grp", "seq"), "mdl", None),
        P("grp", "mdl"),
        P(("mdl", "grp")),
        P(("mdl", "grp")),
        P(("mdl", "grp")),
    )
    chips = mesh.shape["grp"] * mesh.shape["mdl"]
    paired = (
        mesh.shape["seq"] == 2
        and mesh.shape["grp"] == 4
        and KV_HEADS == 2 * mesh.shape["mdl"]
        and HEADS // chips == 4
    )
    return jax.shard_map(
        pair_body if paired else body,
        mesh=mesh,
        in_specs=placed,
        out_specs=(P("seq", ("mdl", "grp")), P("seq", ("mdl", "grp"))),
        check_vma=False,
    )
```

profile of v0, /device:TPU:0, one launch (start us, length us, event | category | flops | bytes accessed | tf_op | source)
XLA Modules:
  0.0 54.2 jit_solution(11164035784038583935)
XLA Ops:
  1.2 3.2 %copy.10 = bf16[1024,2,1280]{2,0,1:T(8,128)(2,1)S(1)} copy(bf16[1024,2,1280]{2,1,0:T(2,128)(2,1)} %param.7) | data formatting | bytes 10485760 | tf_op args[1]
  5.2 0.8 %shard_map.78 = bf16[512,512]{1,0:T(8,128)(2,1)S(1)} custom-call(f32[1]{0:T(128)S(1)} %bitcast.19, bf16[512,2048]{1,0:T(8,128)(2,1)S(1)} %collective-permute-done.x_ref, bf16[2,1024,1280]{2,1,0:T(8,128)(2,1)S(1)} %bitcast.8), custom_call_target="tpu_custom_call" | custom-call | flops 536870912 | bytes 3000000 | tf_op jit(solution)/shard_map/pallas_call | solution.py:299
  6.4 0.8 %shard_map.79 = bf16[512,512]{1,0:T(8,128)(2,1)S(1)} custom-call(f32[1]{0:T(128)S(1)} %bitcast.20, bf16[512,2048]{1,0:T(8,128)(2,1)S(1)} %collective-permute-done.x_ref, bf16[2,1024,1280]{2,1,0:T(8,128)(2,1)S(1)} %bitcast.9), custom_call_target="tpu_custom_call" | custom-call | flops 536870912 | bytes 3000000 | tf_op jit(solution)/shard_map/pallas_call | solution.py:299
  7.4 0.8 %shard_map.80 = bf16[512,512]{1,0:T(8,128)(2,1)S(1)} custom-call(f32[1]{0:T(128)S(1)} %bitcast.21, bf16[512,2048]{1,0:T(8,128)(2,1)S(1)} %collective-permute-done.x_ref, bf16[2,1024,1280]{2,1,0:T(8,128)(2,1)S(1)} %bitcast.10), custom_call_target="tpu_custom_call" | custom-call | flops 536870912 | bytes 3000000 | tf_op jit(solution)/shard_map/pallas_call | solution.py:299
  8.6 0.8 %shard_map.81 = (bf16[544,128]{1,0:T(8,128)(2,1)S(1)}, bf16[512,128]{1,0:T(8,128)(2,1)S(1)}, f32[512,256]{1,0:T(8,128)S(1)}) custom-call(f32[1]{0:T(128)S(1)} %bitcast.22, f32[16,512]{1,0:T(8,128)S(1)} %get-tuple-element.61.raw_ref, bf16[512,2048]{1,0:T(8,128)(2,1)S(1)} %copy-done, bf16[2,1024,1280]{2,1,0:T(8,128)(2,1)S(1)} %bitcast.11, ...), custom_call_target="tpu_custom_call" | custom-call | flops 536870912 | bytes 3000000 | tf_op jit(solution)/shard_map/pallas_call | solution.py:299
  9.4 2.7 %collective-permute-start.4 = (bf16[544,128]{1,0:T(8,128)(2,1)S(1)}, bf16[544,128]{1,0:T(8,128)(2,1)S(1)}, u32[]{:S(2)}, u32[]{:S(2)}) collective-permute-start(bf16[544,128]{1,0:T(8,128)(2,1)S(1)} %get-tuple-element.62), channel_id=1, source_target_pairs={{0,16},{8,24},{16,0},{24,8},{1,17},{9,25},{17,1},{25,9},{2,18},{10... | collective-permute-start | bytes 417800 | tf_op jit(solution)/shard_map/ppermute | solution.py:526
  12.1 0.8 %shard_map.82 = (bf16[512,256]{1,0:T(8,128)(2,1)S(1)}, f32[512,256]{1,0:T(8,128)S(1)}) custom-call(f32[1]{0:T(128)S(1)} %bitcast.23, bf16[512,2048]{1,0:T(8,128)(2,1)S(1)} %copy-done, bf16[2,1024,1280]{2,1,0:T(8,128)(2,1)S(1)} %bitcast.12, bf16[512,512]{1,0:T(8,128)(2,1)S(1)} %collective-permute-done.2.r_ref), custom_call_target="tpu_custom_call" | custom-call | flops 536870912 | bytes 3000000 | tf_op jit(solution)/shard_map/pallas_call | solution.py:299
  12.9 0.8 %shard_map.83 = (bf16[512,256]{1,0:T(8,128)(2,1)S(1)}, f32[512,256]{1,0:T(8,128)S(1)}) custom-call(f32[1]{0:T(128)S(1)} %bitcast.24, bf16[512,2048]{1,0:T(8,128)(2,1)S(1)} %copy-done, bf16[2,1024,1280]{2,1,0:T(8,128)(2,1)S(1)} %bitcast.13, bf16[512,512]{1,0:T(8,128)(2,1)S(1)} %collective-permute-done.3.r_ref), custom_call_target="tpu_custom_call" | custom-call | flops 536870912 | bytes 3000000 | tf_op jit(solution)/shard_map/pallas_call | solution.py:299
  13.7 0.8 %shard_map.84 = bf16[512,512]{1,0:T(8,128)(2,1)S(1)} custom-call(f32[1]{0:T(128)S(1)} %bitcast.25, bf16[512,2048]{1,0:T(8,128)(2,1)S(1)} %collective-permute-done.x_ref, bf16[2,1024,1280]{2,1,0:T(8,128)(2,1)S(1)} %bitcast.14), custom_call_target="tpu_custom_call" | custom-call | flops 536870912 | bytes 3000000 | tf_op jit(solution)/shard_map/pallas_call | solution.py:299
  14.6 1.7 %collective-permute-done.4.u_ref = bf16[544,128]{1,0:T(8,128)(2,1)S(1)} collective-permute-done((bf16[544,128]{1,0:T(8,128)(2,1)S(1)}, bf16[544,128]{1,0:T(8,128)(2,1)S(1)}, u32[]{:S(2)}, u32[]{:S(2)}) %collective-permute-start.4) | collective-permute-done | bytes 139296 | tf_op jit(solution)/shard_map/ppermute | solution.py:526
  16.4 0.8 %shard_map.86 = bf16[512,512]{1,0:T(8,128)(2,1)S(1)} custom-call(f32[1]{0:T(128)S(1)} %bitcast.27, bf16[512,2048]{1,0:T(8,128)(2,1)S(1)} %collective-permute-done.x_ref, bf16[2,1024,1280]{2,1,0:T(8,128)(2,1)S(1)} %bitcast.15), custom_call_target="tpu_custom_call" | custom-call | flops 536870912 | bytes 3000000 | tf_op jit(solution)/shard_map/pallas_call | solution.py:299
  17.3 1.8 %collective-permute-start.7 = (bf16[512,256]{1,0:T(8,128)(2,1)S(1)}, bf16[512,256]{1,0:T(8,128)(2,1)S(1)}, u32[]{:S(2)}, u32[]{:S(2)}) collective-permute-start(bf16[512,256]{1,0:T(8,128)(2,1)S(1)} %get-tuple-element.64), channel_id=1, source_target_pairs={{0,8},{8,0},{16,24},{24,16},{1,9},{9,1},{17,25},{25,17},{2,10},{10... | collective-permute-start | bytes 786440 | tf_op jit(solution)/shard_map/ppermute | solution.py:527
  19.0 1.5 %collective-permute-start.5 = (bf16[512,128]{1,0:T(8,128)(2,1)S(1)}, bf16[512,128]{1,0:T(8,128)(2,1)S(1)}, u32[]{:S(2)}, u32[]{:S(2)}) collective-permute-start(bf16[512,128]{1,0:T(8,128)(2,1)S(1)} %get-tuple-element.72), channel_id=1, source_target_pairs={{0,16},{8,24},{16,0},{24,8},{1,17},{9,25},{17,1},{25,9},{2,18},{10... | collective-permute-start | bytes 393224 | tf_op jit(solution)/shard_map/ppermute | solution.py:526
  21.1 4.3 %collective-permute-done.5.u_ref.u_values_ref = bf16[512,128]{1,0:T(8,128)(2,1)S(1)} collective-permute-done((bf16[512,128]{1,0:T(8,128)(2,1)S(1)}, bf16[512,128]{1,0:T(8,128)(2,1)S(1)}, u32[]{:S(2)}, u32[]{:S(2)}) %collective-permute-start.5) | collective-permute-done | bytes 131104 | tf_op jit(solution)/shard_map/ppermute | solution.py:526
  25.8 1.8 %collective-permute-start.11 = (bf16[512,128]{1,0:T(8,128)(2,1)S(1)}, bf16[512,128]{1,0:T(8,128)(2,1)S(1)}, u32[]{:S(2)}, u32[]{:S(2)}) collective-permute-start(bf16[512,128]{1,0:T(8,128)(2,1)S(1)} %shard_map.87), channel_id=1, source_target_pairs={{0,8},{8,0},{16,24},{24,16},{1,9},{9,1},{17,25},{25,17},{2,10},{10... | collective-permute-start | bytes 393224 | tf_op jit(solution)/shard_map/ppermute | solution.py:527
  27.6 0.8 %shard_map.88 = (bf16[512,256]{1,0:T(8,128)(2,1)S(1)}, f32[512,256]{1,0:T(8,128)S(1)}) custom-call(f32[1]{0:T(128)S(1)} %bitcast.29, bf16[512,2048]{1,0:T(8,128)(2,1)S(1)} %copy-done, bf16[2,1024,1280]{2,1,0:T(8,128)(2,1)S(1)} %bitcast.16, bf16[512,512]{1,0:T(8,128)(2,1)S(1)} %collective-permute-done.6.r_ref), custom_call_target="tpu_custom_call" | custom-call | flops 536870912 | bytes 3000000 | tf_op jit(solution)/shard_map/pallas_call | solution.py:299
  28.5 0.8 %shard_map.90 = (bf16[512,256]{1,0:T(8,128)(2,1)S(1)}, f32[512,256]{1,0:T(8,128)S(1)}) custom-call(f32[1]{0:T(128)S(1)} %bitcast.31, bf16[512,2048]{1,0:T(8,128)(2,1)S(1)} %copy-done, bf16[2,1024,1280]{2,1,0:T(8,128)(2,1)S(1)} %bitcast.17, bf16[512,512]{1,0:T(8,128)(2,1)S(1)} %collective-permute-done.8.r_ref), custom_call_target="tpu_custom_call" | custom-call | flops 536870912 | bytes 3000000 | tf_op jit(solution)/shard_map/pallas_call | solution.py:299
  29.2 1.0 %collective-permute-done.9.u_ref = bf16[512,256]{1,0:T(8,128)(2,1)S(1)} collective-permute-done((bf16[512,256]{1,0:T(8,128)(2,1)S(1)}, bf16[512,256]{1,0:T(8,128)(2,1)S(1)}, u32[]{:S(2)}, u32[]{:S(2)}) %collective-permute-start.9) | collective-permute-done | bytes 262176 | tf_op jit(solution)/shard_map/ppermute | solution.py:526
  30.3 2.0 %collective-permute-done.11.z_values_ref = bf16[512,128]{1,0:T(8,128)(2,1)S(1)} collective-permute-done((bf16[512,128]{1,0:T(8,128)(2,1)S(1)}, bf16[512,128]{1,0:T(8,128)(2,1)S(1)}, u32[]{:S(2)}, u32[]{:S(2)}) %collective-permute-start.11) | collective-permute-done | bytes 131104 | tf_op jit(solution)/shard_map/ppermute | solution.py:527
  32.3 1.3 %shard_map.92 = (bf16[768,256]{1,0:T(8,128)(2,1)S(1)}, bf16[512,128]{1,0:T(8,128)(2,1)S(1)}, f32[8,256]{1,0:T(8,128)S(1)}, f32[256,128]{1,0:T(8,128)S(1)}, f32[8...) custom-call(f32[1]{0:T(128)S(1)} %bitcast.33, f32[16,512]{1,0:T(8,128)S(1)} %get-tuple-element.61.raw_ref, ...), custom_call_target="tpu_custom_call" | custom-call | flops 1000000000 | bytes 3000000 | tf_op jit(solution)/shard_map/pallas_call | solution.py:299
  33.6 1.3 %collective-permute-start.14 = (bf16[512,256]{1,0:T(8,128)(2,1)S(1)}, bf16[512,256]{1,0:T(8,128)(2,1)S(1)}, u32[]{:S(2)}, u32[]{:S(2)}) collective-permute-start(bf16[512,256]{1,0:T(8,128)(2,1)S(1)} %get-tuple-element.74), channel_id=1, source_target_pairs={{0,8},{8,0},{16,24},{24,16},{1,9},{9,1},{17,25},{25,17},{2,10},{10... | collective-permute-start | bytes 786440 | tf_op jit(solution)/shard_map/ppermute | solution.py:527
  34.9 1.5 %collective-permute-start.12 = (bf16[512,128]{1,0:T(8,128)(2,1)S(1)}, bf16[512,128]{1,0:T(8,128)(2,1)S(1)}, u32[]{:S(2)}, u32[]{:S(2)}) collective-permute-start(bf16[512,128]{1,0:T(8,128)(2,1)S(1)} %shard_map.89), channel_id=1, source_target_pairs={{0,16},{8,24},{16,0},{24,8},{1,17},{9,25},{17,1},{25,9},{2,18},{10... | collective-permute-start | bytes 393224 | tf_op jit(solution)/shard_map/ppermute | solution.py:526
  36.9 0.8 %collective-permute-start.16 = (bf16[512,128]{1,0:T(8,128)(2,1)S(1)}, bf16[512,128]{1,0:T(8,128)(2,1)S(1)}, u32[]{:S(2)}, u32[]{:S(2)}) collective-permute-start(bf16[512,128]{1,0:T(8,128)(2,1)S(1)} %shard_map.91), channel_id=1, source_target_pairs={{0,8},{8,0},{16,24},{24,16},{1,9},{9,1},{17,25},{25,17},{2,10},{10... | collective-permute-start | bytes 393224 | tf_op jit(solution)/shard_map/ppermute | solution.py:527
  37.7 3.5 %collective-permute-done.12.z_ref = bf16[512,128]{1,0:T(8,128)(2,1)S(1)} collective-permute-done((bf16[512,128]{1,0:T(8,128)(2,1)S(1)}, bf16[512,128]{1,0:T(8,128)(2,1)S(1)}, u32[]{:S(2)}, u32[]{:S(2)}) %collective-permute-start.12) | collective-permute-done | bytes 131104 | tf_op jit(solution)/shard_map/ppermute | solution.py:526
  41.3 1.4 %shard_map.93 = (bf16[512,128]{1,0:T(8,128)(2,1)S(1)}, bf16[512,128]{1,0:T(8,128)(2,1)S(1)}) custom-call(f32[1]{0:T(128)S(1)} %bitcast.34, f32[512,256]{1,0:T(8,128)S(1)} %get-tuple-element.76.keep_ref, bf16[512,256]{1,0:T(8,128)(2,1)S(1)} %collective-permute-done.7.u_ref, bf16[512,128]{1,0:T(8,128)(2,1)S(1)} %collective-permute-done.12.z_ref, ...), custom_call_target="tpu_custom_call" | custom-call | flops 1000000000 | bytes 3000000 | tf_op jit(solution)/shard_map/pallas_call | solution.py:299
  42.9 1.6 %collective-permute-start.17 = (bf16[512,128]{1,0:T(8,128)(2,1)S(1)}, bf16[512,128]{1,0:T(8,128)(2,1)S(1)}, u32[]{:S(2)}, u32[]{:S(2)}) collective-permute-start(bf16[512,128]{1,0:T(8,128)(2,1)S(1)} %shard_map.94), channel_id=1, source_target_pairs={{0,16},{8,24},{16,0},{24,8},{1,17},{9,25},{17,1},{25,9},{2,18},{10... | collective-permute-start | bytes 393224 | tf_op jit(solution)/shard_map/ppermute | solution.py:526
  44.5 2.4 %collective-permute-done.15.u_ref = bf16[512,256]{1,0:T(8,128)(2,1)S(1)} collective-permute-done((bf16[512,256]{1,0:T(8,128)(2,1)S(1)}, bf16[512,256]{1,0:T(8,128)(2,1)S(1)}, u32[]{:S(2)}, u32[]{:S(2)}) %collective-permute-start.15) | collective-permute-done | bytes 262176 | tf_op jit(solution)/shard_map/ppermute | solution.py:526
  47.0 0.9 %collective-permute-start.18 = (bf16[512,128]{1,0:T(8,128)(2,1)S(1)}, bf16[512,128]{1,0:T(8,128)(2,1)S(1)}, u32[]{:S(2)}, u32[]{:S(2)}) collective-permute-start(bf16[512,128]{1,0:T(8,128)(2,1)S(1)} %shard_map.95), channel_id=1, source_target_pairs={{0,8},{8,0},{16,24},{24,16},{1,9},{9,1},{17,25},{25,17},{2,10},{10... | collective-permute-start | bytes 393224 | tf_op jit(solution)/shard_map/ppermute | solution.py:527
  47.9 1.4 %shard_map.96 = (bf16[512,128]{1,0:T(8,128)(2,1)S(1)}, bf16[512,128]{1,0:T(8,128)(2,1)S(1)}) custom-call(f32[1]{0:T(128)S(1)} %bitcast.38, f32[512,256]{1,0:T(8,128)S(1)} %get-tuple-element.80.keep_ref, bf16[512,256]{1,0:T(8,128)(2,1)S(1)} %collective-permute-done.9.u_ref, bf16[512,128]{1,0:T(8,128)(2,1)S(1)} %collective-permute-done.16.z_ref, ...), custom_call_target="tpu_custom_call" | custom-call | flops 1000000000 | bytes 3000000 | tf_op jit(solution)/shard_map/pallas_call | solution.py:299
  49.3 1.4 %shard_map.97 = (bf16[512,128]{1,0:T(8,128)(2,1)S(1)}, bf16[512,128]{1,0:T(8,128)(2,1)S(1)}) custom-call(f32[1]{0:T(128)S(1)} %bitcast.40, f32[512,256]{1,0:T(8,128)S(1)} %get-tuple-element.93.keep_ref, bf16[512,256]{1,0:T(8,128)(2,1)S(1)} %collective-permute-done.14.u_ref, bf16[512,128]{1,0:T(8,128)(2,1)S(1)} %collective-permute-done.17.z_ref, ...), custom_call_target="tpu_custom_call" | custom-call | flops 1000000000 | bytes 3000000 | tf_op jit(solution)/shard_map/pallas_call | solution.py:299
  50.7 1.3 %collective-permute-done.18.z_ref = bf16[512,128]{1,0:T(8,128)(2,1)S(1)} collective-permute-done((bf16[512,128]{1,0:T(8,128)(2,1)S(1)}, bf16[512,128]{1,0:T(8,128)(2,1)S(1)}, u32[]{:S(2)}, u32[]{:S(2)}) %collective-permute-start.18) | collective-permute-done | bytes 131104 | tf_op jit(solution)/shard_map/ppermute | solution.py:527
  52.0 2.2 %shard_map.98 = (bf16[512,512]{1,0:T(8,128)(2,1)}, bf16[512,512]{1,0:T(8,128)(2,1)}) custom-call(f32[1]{0:T(128)S(1)} %bitcast.42, f32[512,256]{1,0:T(8,128)S(1)} %get-tuple-element.95.keep_ref, bf16[512,256]{1,0:T(8,128)(2,1)S(1)} %collective-permute-done.15.u_ref, bf16[512,128]{1,0:T(8,128)(2,1)S(1)} %collective-permute-done.18.z_ref, ...), custom_call_target="tpu_custom_call" | custom-call | flops 1000000000 | bytes 3000000 | tf_op jit(solution)/shard_map/pallas_call | solution.py:299
  (39 shorter events, 4.7 us)
Async XLA Ops:
  0.6 3.8 %copy-start = (bf16[512,2048]{1,0:T(8,128)(2,1)S(1)}, bf16[512,2048]{1,0:T(8,128)(2,1)}, u32[]{:S(2)}) copy-start(bf16[512,2048]{1,0:T(8,128)(2,1)} %x_ref.11) | copy-start | bytes 6291460
  0.6 3.8 %copy-start.1 = (f32[4]{0:T(128)S(1)}, f32[4]{0:T(128)}, u32[]{:S(2)}) copy-start(f32[4]{0:T(128)} %param.11) | copy-start | bytes 52
  0.7 3.8 %copy-start.2 = (bf16[2048,16]{0,1:T(8,128)(2,1)S(1)}, bf16[2048,16]{0,1:T(8,128)(2,1)}, u32[]{:S(2)}) copy-start(bf16[2048,16]{0,1:T(8,128)(2,1)} %param.8) | copy-start | bytes 196612
  0.7 4.6 %collective-permute-start = (bf16[512,2048]{1,0:T(8,128)(2,1)}, bf16[512,2048]{1,0:T(8,128)(2,1)S(1)}, u32[]{:S(2)}, u32[]{:S(2)}) collective-permute-start(bf16[512,2048]{1,0:T(8,128)(2,1)} %x_ref.11), channel_id=1, source_target_pairs={{0,4},{4,0},{1,5},{5,1},{2,6},{6,2},{3,7},{7,3},{8,12},{12,8},{9,1... | collective-permute-start | bytes 6291464 | tf_op jit(solution)/shard_map/ppermute | solution.py:528
  6.0 2.7 %collective-permute-start.1 = (bf16[512,512]{1,0:T(8,128)(2,1)S(1)}, bf16[512,512]{1,0:T(8,128)(2,1)S(1)}, u32[]{:S(2)}, u32[]{:S(2)}) collective-permute-start(bf16[512,512]{1,0:T(8,128)(2,1)S(1)} %shard_map.78), channel_id=1, source_target_pairs={{0,4},{4,0},{1,5},{5,1},{2,6},{6,2},{3,7},{7,3},{8,12},{12,8},{9,1... | collective-permute-start | bytes 1572872 | tf_op jit(solution)/shard_map/ppermute | solution.py:528
  7.2 4.9 %collective-permute-start.2 = (bf16[512,512]{1,0:T(8,128)(2,1)S(1)}, bf16[512,512]{1,0:T(8,128)(2,1)S(1)}, u32[]{:S(2)}, u32[]{:S(2)}) collective-permute-start(bf16[512,512]{1,0:T(8,128)(2,1)S(1)} %shard_map.79), channel_id=1, source_target_pairs={{0,4},{4,0},{1,5},{5,1},{2,6},{6,2},{3,7},{7,3},{8,12},{12,8},{9,1... | collective-permute-start | bytes 1572872 | tf_op jit(solution)/shard_map/ppermute | solution.py:528
  8.2 4.7 %collective-permute-start.3 = (bf16[512,512]{1,0:T(8,128)(2,1)S(1)}, bf16[512,512]{1,0:T(8,128)(2,1)S(1)}, u32[]{:S(2)}, u32[]{:S(2)}) collective-permute-start(bf16[512,512]{1,0:T(8,128)(2,1)S(1)} %shard_map.80), channel_id=1, source_target_pairs={{0,4},{4,0},{1,5},{5,1},{2,6},{6,2},{3,7},{7,3},{8,12},{12,8},{9,1... | collective-permute-start | bytes 1572872 | tf_op jit(solution)/shard_map/ppermute | solution.py:528
  9.4 6.9 %collective-permute-start.4 = (bf16[544,128]{1,0:T(8,128)(2,1)S(1)}, bf16[544,128]{1,0:T(8,128)(2,1)S(1)}, u32[]{:S(2)}, u32[]{:S(2)}) collective-permute-start(bf16[544,128]{1,0:T(8,128)(2,1)S(1)} %get-tuple-element.62), channel_id=1, source_target_pairs={{0,16},{8,24},{16,0},{24,8},{1,17},{9,25},{17,1},{25,9},{2,18},{10... | collective-permute-start | bytes 417800 | tf_op jit(solution)/shard_map/ppermute | solution.py:526
  14.5 11.3 %collective-permute-start.6 = (bf16[512,512]{1,0:T(8,128)(2,1)S(1)}, bf16[512,512]{1,0:T(8,128)(2,1)S(1)}, u32[]{:S(2)}, u32[]{:S(2)}) collective-permute-start(bf16[512,512]{1,0:T(8,128)(2,1)S(1)} %shard_map.84), channel_id=1, source_target_pairs={{0,4},{4,0},{1,5},{5,1},{2,6},{6,2},{3,7},{7,3},{8,12},{12,8},{9,1... | collective-permute-start | bytes 1572872 | tf_op jit(solution)/shard_map/ppermute | solution.py:528
  17.2 11.3 %collective-permute-start.8 = (bf16[512,512]{1,0:T(8,128)(2,1)S(1)}, bf16[512,512]{1,0:T(8,128)(2,1)S(1)}, u32[]{:S(2)}, u32[]{:S(2)}) collective-permute-start(bf16[512,512]{1,0:T(8,128)(2,1)S(1)} %shard_map.86), channel_id=1, source_target_pairs={{0,4},{4,0},{1,5},{5,1},{2,6},{6,2},{3,7},{7,3},{8,12},{12,8},{9,1... | collective-permute-start | bytes 1572872 | tf_op jit(solution)/shard_map/ppermute | solution.py:528
  17.3 11.1 %collective-permute-start.7 = (bf16[512,256]{1,0:T(8,128)(2,1)S(1)}, bf16[512,256]{1,0:T(8,128)(2,1)S(1)}, u32[]{:S(2)}, u32[]{:S(2)}) collective-permute-start(bf16[512,256]{1,0:T(8,128)(2,1)S(1)} %get-tuple-element.64), channel_id=1, source_target_pairs={{0,8},{8,0},{16,24},{24,16},{1,9},{9,1},{17,25},{25,17},{2,10},{10... | collective-permute-start | bytes 786440 | tf_op jit(solution)/shard_map/ppermute | solution.py:527
  19.0 6.4 %collective-permute-start.5 = (bf16[512,128]{1,0:T(8,128)(2,1)S(1)}, bf16[512,128]{1,0:T(8,128)(2,1)S(1)}, u32[]{:S(2)}, u32[]{:S(2)}) collective-permute-start(bf16[512,128]{1,0:T(8,128)(2,1)S(1)} %get-tuple-element.72), channel_id=1, source_target_pairs={{0,16},{8,24},{16,0},{24,8},{1,17},{9,25},{17,1},{25,9},{2,18},{10... | collective-permute-start | bytes 393224 | tf_op jit(solution)/shard_map/ppermute | solution.py:526
  20.6 9.7 %collective-permute-start.9 = (bf16[512,256]{1,0:T(8,128)(2,1)S(1)}, bf16[512,256]{1,0:T(8,128)(2,1)S(1)}, u32[]{:S(2)}, u32[]{:S(2)}) collective-permute-start(bf16[512,256]{1,0:T(8,128)(2,1)S(1)} %get-tuple-element.66), channel_id=1, source_target_pairs={{0,16},{8,24},{16,0},{24,8},{1,17},{9,25},{17,1},{25,9},{2,18},{10... | collective-permute-start | bytes 786440 | tf_op jit(solution)/shard_map/ppermute | solution.py:526
  25.4 6.9 %collective-permute-start.10 = (bf16[544,128]{1,0:T(8,128)(2,1)S(1)}, bf16[544,128]{1,0:T(8,128)(2,1)S(1)}, u32[]{:S(2)}, u32[]{:S(2)}) collective-permute-start(bf16[544,128]{1,0:T(8,128)(2,1)S(1)} %shard_map.85), channel_id=1, source_target_pairs={{0,8},{8,0},{16,24},{24,16},{1,9},{9,1},{17,25},{25,17},{2,10},{10... | collective-permute-start | bytes 417800 | tf_op jit(solution)/shard_map/ppermute | solution.py:527
  25.8 6.5 %collective-permute-start.11 = (bf16[512,128]{1,0:T(8,128)(2,1)S(1)}, bf16[512,128]{1,0:T(8,128)(2,1)S(1)}, u32[]{:S(2)}, u32[]{:S(2)}) collective-permute-start(bf16[512,128]{1,0:T(8,128)(2,1)S(1)} %shard_map.87), channel_id=1, source_target_pairs={{0,8},{8,0},{16,24},{24,16},{1,9},{9,1},{17,25},{25,17},{2,10},{10... | collective-permute-start | bytes 393224 | tf_op jit(solution)/shard_map/ppermute | solution.py:527
  28.4 3.9 %copy-start.3 = (f32[4]{0:T(128)S(1)}, f32[4]{0:T(128)}, u32[]{:S(2)}) copy-start(f32[4]{0:T(128)} %param.9) | copy-start | bytes 52
  28.4 3.9 %copy-start.4 = (f32[4]{0:T(128)S(1)}, f32[4]{0:T(128)}, u32[]{:S(2)}) copy-start(f32[4]{0:T(128)} %param.10) | copy-start | bytes 52
  33.5 7.7 %collective-permute-start.13 = (bf16[768,256]{1,0:T(8,128)(2,1)S(1)}, bf16[768,256]{1,0:T(8,128)(2,1)S(1)}, u32[]{:S(2)}, u32[]{:S(2)}) collective-permute-start(bf16[768,256]{1,0:T(8,128)(2,1)S(1)} %get-tuple-element.84.carry_ref), channel_id=1, source_target_pairs={{0,4},{4,0},{1,5},{5,1},{2,6},{6,2},{3,7},{7,3},{8,12},{12,8},{9,1... | collective-permute-start | bytes 1179656 | tf_op jit(solution)/shard_map/ppermute | solution.py:528
  33.6 9.2 %collective-permute-start.14 = (bf16[512,256]{1,0:T(8,128)(2,1)S(1)}, bf16[512,256]{1,0:T(8,128)(2,1)S(1)}, u32[]{:S(2)}, u32[]{:S(2)}) collective-permute-start(bf16[512,256]{1,0:T(8,128)(2,1)S(1)} %get-tuple-element.74), channel_id=1, source_target_pairs={{0,8},{8,0},{16,24},{24,16},{1,9},{9,1},{17,25},{25,17},{2,10},{10... | collective-permute-start | bytes 786440 | tf_op jit(solution)/shard_map/ppermute | solution.py:527
  34.9 6.4 %collective-permute-start.12 = (bf16[512,128]{1,0:T(8,128)(2,1)S(1)}, bf16[512,128]{1,0:T(8,128)(2,1)S(1)}, u32[]{:S(2)}, u32[]{:S(2)}) collective-permute-start(bf16[512,128]{1,0:T(8,128)(2,1)S(1)} %shard_map.89), channel_id=1, source_target_pairs={{0,16},{8,24},{16,0},{24,8},{1,17},{9,25},{17,1},{25,9},{2,18},{10... | collective-permute-start | bytes 393224 | tf_op jit(solution)/shard_map/ppermute | solution.py:526
  36.4 10.5 %collective-permute-start.15 = (bf16[512,256]{1,0:T(8,128)(2,1)S(1)}, bf16[512,256]{1,0:T(8,128)(2,1)S(1)}, u32[]{:S(2)}, u32[]{:S(2)}) collective-permute-start(bf16[512,256]{1,0:T(8,128)(2,1)S(1)} %get-tuple-element.78), channel_id=1, source_target_pairs={{0,16},{8,24},{16,0},{24,8},{1,17},{9,25},{17,1},{25,9},{2,18},{10... | collective-permute-start | bytes 786440 | tf_op jit(solution)/shard_map/ppermute | solution.py:526
  36.9 10.9 %collective-permute-start.16 = (bf16[512,128]{1,0:T(8,128)(2,1)S(1)}, bf16[512,128]{1,0:T(8,128)(2,1)S(1)}, u32[]{:S(2)}, u32[]{:S(2)}) collective-permute-start(bf16[512,128]{1,0:T(8,128)(2,1)S(1)} %shard_map.91), channel_id=1, source_target_pairs={{0,8},{8,0},{16,24},{24,16},{1,9},{9,1},{17,25},{25,17},{2,10},{10... | collective-permute-start | bytes 393224 | tf_op jit(solution)/shard_map/ppermute | solution.py:527
  42.9 6.3 %collective-permute-start.17 = (bf16[512,128]{1,0:T(8,128)(2,1)S(1)}, bf16[512,128]{1,0:T(8,128)(2,1)S(1)}, u32[]{:S(2)}, u32[]{:S(2)}) collective-permute-start(bf16[512,128]{1,0:T(8,128)(2,1)S(1)} %shard_map.94), channel_id=1, source_target_pairs={{0,16},{8,24},{16,0},{24,8},{1,17},{9,25},{17,1},{25,9},{2,18},{10... | collective-permute-start | bytes 393224 | tf_op jit(solution)/shard_map/ppermute | solution.py:526
  47.0 5.0 %collective-permute-start.18 = (bf16[512,128]{1,0:T(8,128)(2,1)S(1)}, bf16[512,128]{1,0:T(8,128)(2,1)S(1)}, u32[]{:S(2)}, u32[]{:S(2)}) collective-permute-start(bf16[512,128]{1,0:T(8,128)(2,1)S(1)} %shard_map.95), channel_id=1, source_target_pairs={{0,8},{8,0},{16,24},{24,16},{1,9},{9,1},{17,25},{25,17},{2,10},{10... | collective-permute-start | bytes 393224 | tf_op jit(solution)/shard_map/ppermute | solution.py:527
where the time goes:
time: 54.3 us; the launch traced here: 54.2 us
  starting transfers between devices  17.1 us (31%)
  Pallas kernels  16.6 us (31%)
  waiting for transfers between devices  16.4 us (30%)
  local copies, waits for them, and re-layouts  3.25 us (6%)
  between operations  0.91 us (2%)
    pallas_call x22, Pallas kernels, call(): pl.pallas_call(kernel, in_specs=[ANY] + (in_specs or [VMEM] * len(args)),...  16.6 us
    ppermute x6, waiting for transfers between devices, pair_steps(): over_high = lambda a: lax.ppermute(a, 'grp', swap_high)  12.9 us
    ppermute x6, starting transfers between devices, pair_steps(): over_high = lambda a: lax.ppermute(a, 'grp', swap_high)  8.32 us
    ppermute x6, starting transfers between devices, pair_steps(): over_low = lambda a: lax.ppermute(a, 'grp', swap_low)  6.86 us
    ppermute x6, waiting for transfers between devices, pair_steps(): over_low = lambda a: lax.ppermute(a, 'grp', swap_low)  3.45 us
    unnamed x11, local copies, waits for them, and re-layouts  3.25 us
    ppermute x7, starting transfers between devices, pair_steps(): over_seq = lambda a: lax.ppermute(a, 'seq', [(0, 1), (1, 0)])  1.95 us
  transfers between devices with their start and end apart: 19, of which 8 were waited for; matrix products, arithmetic and copies ran while one was open for 6% of the time, Pallas kernels for 23%

commit v1 on v0

--- a/solution.py
+++ b/solution.py
@@ -636,16 +636,14 @@
     cross(4)
     middle("v")
     mine(3)
+    mine(4)
     middle(1)
-    mine(4)
     middle(2)
     shared = context()
-    done = {1: tail(1, shared, None)}
+    middle(4)
     middle(3)
-    middle(4)
-    for j in (0, 3):
-        done[j] = tail(j, shared, None)
-    outs = tail(2, shared, [part for j in sorted(done) for part in done[j]])
+    done = {j: tail(j, shared, None) for j in (0, 1, 2)}
+    outs = tail(3, shared, [part for j in sorted(done) for part in done[j]])
     return outs[0], outs[1]
 
 

time: 54.3 us -> 53.2 us (0.980)
  waiting for transfers between devices: 16.4 us -> 15.5 us
    ppermute x6, waiting for transfers between devices: 12.9 us -> 9.51 us  [pair_steps(): over_high = lambda a: lax.ppermute(a, 'grp', swap_high)]
    ppermute x6, waiting for transfers between devices: 3.45 us -> 5.98 us  [pair_steps(): over_low = lambda a: lax.ppermute(a, 'grp', swap_low)]
    ppermute x6, starting transfers between devices: 8.32 us -> 7.68 us  [pair_steps(): over_high = lambda a: lax.ppermute(a, 'grp', swap_high)]
  transfers between devices with their start and end apart: 19 -> 19, of which waited for: 8 -> 7; matrix products, arithmetic and copies ran while one was open for 6% -> 6% of each run, Pallas kernels for 23% -> 23%
where the time goes in v1:
time: 53.2 us; the launch traced here: 53.1 us
  starting transfers between devices  16.9 us (32%)
  Pallas kernels  16.5 us (31%)
  waiting for transfers between devices  15.5 us (29%)
  local copies, waits for them, and re-layouts  3.25 us (6%)
  between operations  0.93 us (2%)
    pallas_call x22, Pallas kernels, call(): pl.pallas_call(kernel, in_specs=[ANY] + (in_specs or [VMEM] * len(args)),...  16.5 us
    ppermute x6, waiting for transfers between devices, pair_steps(): over_high = lambda a: lax.ppermute(a, 'grp', swap_high)  9.51 us
    ppermute x6, starting transfers between devices, pair_steps(): over_high = lambda a: lax.ppermute(a, 'grp', swap_high)  7.68 us
    ppermute x6, starting transfers between devices, pair_steps(): over_low = lambda a: lax.ppermute(a, 'grp', swap_low)  7.25 us
    ppermute x6, waiting for transfers between devices, pair_steps(): over_low = lambda a: lax.ppermute(a, 'grp', swap_low)  5.98 us
    unnamed x11, local copies, waits for them, and re-layouts  3.25 us
    ppermute x7, starting transfers between devices, pair_steps(): over_seq = lambda a: lax.ppermute(a, 'seq', [(0, 1), (1, 0)])  1.95 us
  transfers between devices with their start and end apart: 19, of which 7 were waited for; matrix products, arithmetic and copies ran while one was open for 6% of the time, Pallas kernels for 23%

profile of v1, /device:TPU:0, one launch (start us, length us, event | category | flops | bytes accessed | tf_op | source)
XLA Modules:
  0.0 53.1 jit_solution(17468482476485946280)
XLA Ops:
  0.7 0.6 %collective-permute-start = (bf16[512,2048]{1,0:T(8,128)(2,1)}, bf16[512,2048]{1,0:T(8,128)(2,1)S(1)}, u32[]{:S(2)}, u32[]{:S(2)}) collective-permute-start(bf16[512,2048]{1,0:T(8,128)(2,1)} %x_ref.11), channel_id=1, source_target_pairs={{0,4},{4,0},{1,5},{5,1},{2,6},{6,2},{3,7},{7,3},{8,12},{12,8},{9,1... | collective-permute-start | bytes 6291464 | tf_op jit(solution)/shard_map/ppermute | solution.py:528
  1.2 3.2 %copy.10 = bf16[1024,2,1280]{2,0,1:T(8,128)(2,1)S(1)} copy(bf16[1024,2,1280]{2,1,0:T(2,128)(2,1)} %param.7) | data formatting | bytes 10485760 | tf_op args[1]
  4.5 0.7 %shard_map.77 = (f32[16,512]{1,0:T(8,128)S(1)}, f32[512,128]{1,0:T(8,128)S(1)}, f32[512,128]{1,0:T(8,128)S(1)}) custom-call(f32[1]{0:T(128)S(1)} %bitcast.18, bf16[512,2048]{1,0:T(8,128)(2,1)S(1)} %copy-done, bf16[16,2048]{1,0:T(8,128)(2,1)S(1)} %bitcast.44), custom_call_target="tpu_custom_call" | custom-call | flops 1000000000 | bytes 3000000 | tf_op jit(solution)/shard_map/pallas_call | solution.py:299
  5.2 0.8 %shard_map.78 = bf16[512,512]{1,0:T(8,128)(2,1)S(1)} custom-call(f32[1]{0:T(128)S(1)} %bitcast.19, bf16[512,2048]{1,0:T(8,128)(2,1)S(1)} %collective-permute-done.x_ref, bf16[2,1024,1280]{2,1,0:T(8,128)(2,1)S(1)} %bitcast.8), custom_call_target="tpu_custom_call" | custom-call | flops 536870912 | bytes 3000000 | tf_op jit(solution)/shard_map/pallas_call | solution.py:299
  6.4 0.8 %shard_map.79 = bf16[512,512]{1,0:T(8,128)(2,1)S(1)} custom-call(f32[1]{0:T(128)S(1)} %bitcast.20, bf16[512,2048]{1,0:T(8,128)(2,1)S(1)} %collective-permute-done.x_ref, bf16[2,1024,1280]{2,1,0:T(8,128)(2,1)S(1)} %bitcast.9), custom_call_target="tpu_custom_call" | custom-call | flops 536870912 | bytes 3000000 | tf_op jit(solution)/shard_map/pallas_call | solution.py:299
  7.4 0.8 %shard_map.80 = bf16[512,512]{1,0:T(8,128)(2,1)S(1)} custom-call(f32[1]{0:T(128)S(1)} %bitcast.21, bf16[512,2048]{1,0:T(8,128)(2,1)S(1)} %collective-permute-done.x_ref, bf16[2,1024,1280]{2,1,0:T(8,128)(2,1)S(1)} %bitcast.10), custom_call_target="tpu_custom_call" | custom-call | flops 536870912 | bytes 3000000 | tf_op jit(solution)/shard_map/pallas_call | solution.py:299
  8.6 0.8 %shard_map.81 = (bf16[544,128]{1,0:T(8,128)(2,1)S(1)}, bf16[512,128]{1,0:T(8,128)(2,1)S(1)}, f32[512,256]{1,0:T(8,128)S(1)}) custom-call(f32[1]{0:T(128)S(1)} %bitcast.22, f32[16,512]{1,0:T(8,128)S(1)} %get-tuple-element.61.raw_ref, bf16[512,2048]{1,0:T(8,128)(2,1)S(1)} %copy-done, bf16[2,1024,1280]{2,1,0:T(8,128)(2,1)S(1)} %bitcast.11, ...), custom_call_target="tpu_custom_call" | custom-call | flops 536870912 | bytes 3000000 | tf_op jit(solution)/shard_map/pallas_call | solution.py:299
  9.4 2.7 %collective-permute-start.4 = (bf16[544,128]{1,0:T(8,128)(2,1)S(1)}, bf16[544,128]{1,0:T(8,128)(2,1)S(1)}, u32[]{:S(2)}, u32[]{:S(2)}) collective-permute-start(bf16[544,128]{1,0:T(8,128)(2,1)S(1)} %get-tuple-element.62), channel_id=1, source_target_pairs={{0,16},{8,24},{16,0},{24,8},{1,17},{9,25},{17,1},{25,9},{2,18},{10... | collective-permute-start | bytes 417800 | tf_op jit(solution)/shard_map/ppermute | solution.py:526
  12.1 0.8 %shard_map.82 = (bf16[512,256]{1,0:T(8,128)(2,1)S(1)}, f32[512,256]{1,0:T(8,128)S(1)}) custom-call(f32[1]{0:T(128)S(1)} %bitcast.23, bf16[512,2048]{1,0:T(8,128)(2,1)S(1)} %copy-done, bf16[2,1024,1280]{2,1,0:T(8,128)(2,1)S(1)} %bitcast.12, bf16[512,512]{1,0:T(8,128)(2,1)S(1)} %collective-permute-done.2.r_ref), custom_call_target="tpu_custom_call" | custom-call | flops 536870912 | bytes 3000000 | tf_op jit(solution)/shard_map/pallas_call | solution.py:299
  12.9 0.8 %shard_map.83 = (bf16[512,256]{1,0:T(8,128)(2,1)S(1)}, f32[512,256]{1,0:T(8,128)S(1)}) custom-call(f32[1]{0:T(128)S(1)} %bitcast.24, bf16[512,2048]{1,0:T(8,128)(2,1)S(1)} %copy-done, bf16[2,1024,1280]{2,1,0:T(8,128)(2,1)S(1)} %bitcast.13, bf16[512,512]{1,0:T(8,128)(2,1)S(1)} %collective-permute-done.3.r_ref), custom_call_target="tpu_custom_call" | custom-call | flops 536870912 | bytes 3000000 | tf_op jit(solution)/shard_map/pallas_call | solution.py:299
  13.7 0.8 %shard_map.84 = bf16[512,512]{1,0:T(8,128)(2,1)S(1)} custom-call(f32[1]{0:T(128)S(1)} %bitcast.25, bf16[512,2048]{1,0:T(8,128)(2,1)S(1)} %collective-permute-done.x_ref, bf16[2,1024,1280]{2,1,0:T(8,128)(2,1)S(1)} %bitcast.14), custom_call_target="tpu_custom_call" | custom-call | flops 536870912 | bytes 3000000 | tf_op jit(solution)/shard_map/pallas_call | solution.py:299
  14.6 1.7 %collective-permute-done.4.u_ref = bf16[544,128]{1,0:T(8,128)(2,1)S(1)} collective-permute-done((bf16[544,128]{1,0:T(8,128)(2,1)S(1)}, bf16[544,128]{1,0:T(8,128)(2,1)S(1)}, u32[]{:S(2)}, u32[]{:S(2)}) %collective-permute-start.4) | collective-permute-done | bytes 139296 | tf_op jit(solution)/shard_map/ppermute | solution.py:526
  16.4 0.8 %shard_map.86 = bf16[512,512]{1,0:T(8,128)(2,1)S(1)} custom-call(f32[1]{0:T(128)S(1)} %bitcast.27, bf16[512,2048]{1,0:T(8,128)(2,1)S(1)} %collective-permute-done.x_ref, bf16[2,1024,1280]{2,1,0:T(8,128)(2,1)S(1)} %bitcast.15), custom_call_target="tpu_custom_call" | custom-call | flops 536870912 | bytes 3000000 | tf_op jit(solution)/shard_map/pallas_call | solution.py:299
  17.3 1.8 %collective-permute-start.5 = (bf16[512,128]{1,0:T(8,128)(2,1)S(1)}, bf16[512,128]{1,0:T(8,128)(2,1)S(1)}, u32[]{:S(2)}, u32[]{:S(2)}) collective-permute-start(bf16[512,128]{1,0:T(8,128)(2,1)S(1)} %get-tuple-element.72), channel_id=1, source_target_pairs={{0,16},{8,24},{16,0},{24,8},{1,17},{9,25},{17,1},{25,9},{2,18},{10... | collective-permute-start | bytes 393224 | tf_op jit(solution)/shard_map/ppermute | solution.py:526
  19.1 1.5 %collective-permute-start.8 = (bf16[512,256]{1,0:T(8,128)(2,1)S(1)}, bf16[512,256]{1,0:T(8,128)(2,1)S(1)}, u32[]{:S(2)}, u32[]{:S(2)}) collective-permute-start(bf16[512,256]{1,0:T(8,128)(2,1)S(1)} %get-tuple-element.64), channel_id=1, source_target_pairs={{0,8},{8,0},{16,24},{24,16},{1,9},{9,1},{17,25},{25,17},{2,10},{10... | collective-permute-start | bytes 786440 | tf_op jit(solution)/shard_map/ppermute | solution.py:527
  20.6 0.5 collective-permute-start.9
  21.1 2.2 %collective-permute-done.5.u_ref.u_values_ref = bf16[512,128]{1,0:T(8,128)(2,1)S(1)} collective-permute-done((bf16[512,128]{1,0:T(8,128)(2,1)S(1)}, bf16[512,128]{1,0:T(8,128)(2,1)S(1)}, u32[]{:S(2)}, u32[]{:S(2)}) %collective-permute-start.5) | collective-permute-done | bytes 131104 | tf_op jit(solution)/shard_map/ppermute | solution.py:526
  23.3 2.1 %collective-permute-start.10 = (bf16[544,128]{1,0:T(8,128)(2,1)S(1)}, bf16[544,128]{1,0:T(8,128)(2,1)S(1)}, u32[]{:S(2)}, u32[]{:S(2)}) collective-permute-start(bf16[544,128]{1,0:T(8,128)(2,1)S(1)} %shard_map.85), channel_id=1, source_target_pairs={{0,8},{8,0},{16,24},{24,16},{1,9},{9,1},{17,25},{25,17},{2,10},{10... | collective-permute-start | bytes 417800 | tf_op jit(solution)/shard_map/ppermute | solution.py:527
  25.6 0.8 %shard_map.88 = (bf16[512,256]{1,0:T(8,128)(2,1)S(1)}, f32[512,256]{1,0:T(8,128)S(1)}) custom-call(f32[1]{0:T(128)S(1)} %bitcast.29, bf16[512,2048]{1,0:T(8,128)(2,1)S(1)} %copy-done, bf16[2,1024,1280]{2,1,0:T(8,128)(2,1)S(1)} %bitcast.16, bf16[512,512]{1,0:T(8,128)(2,1)S(1)} %collective-permute-done.6.r_ref), custom_call_target="tpu_custom_call" | custom-call | flops 536870912 | bytes 3000000 | tf_op jit(solution)/shard_map/pallas_call | solution.py:299
  26.4 0.8 %shard_map.89 = (bf16[512,256]{1,0:T(8,128)(2,1)S(1)}, f32[512,256]{1,0:T(8,128)S(1)}) custom-call(f32[1]{0:T(128)S(1)} %bitcast.30, bf16[512,2048]{1,0:T(8,128)(2,1)S(1)} %copy-done, bf16[2,1024,1280]{2,1,0:T(8,128)(2,1)S(1)} %bitcast.17, bf16[512,512]{1,0:T(8,128)(2,1)S(1)} %collective-permute-done.7.r_ref), custom_call_target="tpu_custom_call" | custom-call | flops 536870912 | bytes 3000000 | tf_op jit(solution)/shard_map/pallas_call | solution.py:299
  27.2 1.1 %collective-permute-done.8.u_ref = bf16[512,256]{1,0:T(8,128)(2,1)S(1)} collective-permute-done((bf16[512,256]{1,0:T(8,128)(2,1)S(1)}, bf16[512,256]{1,0:T(8,128)(2,1)S(1)}, u32[]{:S(2)}, u32[]{:S(2)}) %collective-permute-start.8) | collective-permute-done | bytes 262176 | tf_op jit(solution)/shard_map/ppermute | solution.py:527
  28.8 4.4 %collective-permute-done.11.z_values_ref = bf16[512,128]{1,0:T(8,128)(2,1)S(1)} collective-permute-done((bf16[512,128]{1,0:T(8,128)(2,1)S(1)}, bf16[512,128]{1,0:T(8,128)(2,1)S(1)}, u32[]{:S(2)}, u32[]{:S(2)}) %collective-permute-start.11) | collective-permute-done | bytes 131104 | tf_op jit(solution)/shard_map/ppermute | solution.py:527
  33.2 1.3 %shard_map.92 = (bf16[768,256]{1,0:T(8,128)(2,1)S(1)}, bf16[512,128]{1,0:T(8,128)(2,1)S(1)}, f32[8,256]{1,0:T(8,128)S(1)}, f32[256,128]{1,0:T(8,128)S(1)}, f32[8...) custom-call(f32[1]{0:T(128)S(1)} %bitcast.33, f32[16,512]{1,0:T(8,128)S(1)} %get-tuple-element.61.raw_ref, ...), custom_call_target="tpu_custom_call" | custom-call | flops 1000000000 | bytes 3000000 | tf_op jit(solution)/shard_map/pallas_call | solution.py:299
  34.9 1.7 %collective-permute-start.13 = (bf16[512,256]{1,0:T(8,128)(2,1)S(1)}, bf16[512,256]{1,0:T(8,128)(2,1)S(1)}, u32[]{:S(2)}, u32[]{:S(2)}) collective-permute-start(bf16[512,256]{1,0:T(8,128)(2,1)S(1)} %get-tuple-element.74), channel_id=1, source_target_pairs={{0,8},{8,0},{16,24},{24,16},{1,9},{9,1},{17,25},{25,17},{2,10},{10... | collective-permute-start | bytes 786440 | tf_op jit(solution)/shard_map/ppermute | solution.py:527
  36.9 1.7 %collective-permute-start.16 = (bf16[512,128]{1,0:T(8,128)(2,1)S(1)}, bf16[512,128]{1,0:T(8,128)(2,1)S(1)}, u32[]{:S(2)}, u32[]{:S(2)}) collective-permute-start(bf16[512,128]{1,0:T(8,128)(2,1)S(1)} %shard_map.90), channel_id=1, source_target_pairs={{0,16},{8,24},{16,0},{24,8},{1,17},{9,25},{17,1},{25,9},{2,18},{10... | collective-permute-start | bytes 393224 | tf_op jit(solution)/shard_map/ppermute | solution.py:526
  38.7 5.1 %collective-permute-done.12.u_ref = bf16[512,256]{1,0:T(8,128)(2,1)S(1)} collective-permute-done((bf16[512,256]{1,0:T(8,128)(2,1)S(1)}, bf16[512,256]{1,0:T(8,128)(2,1)S(1)}, u32[]{:S(2)}, u32[]{:S(2)}) %collective-permute-start.12) | collective-permute-done | bytes 262176 | tf_op jit(solution)/shard_map/ppermute | solution.py:526
  43.9 1.6 %collective-permute-start.17 = (bf16[512,128]{1,0:T(8,128)(2,1)S(1)}, bf16[512,128]{1,0:T(8,128)(2,1)S(1)}, u32[]{:S(2)}, u32[]{:S(2)}) collective-permute-start(bf16[512,128]{1,0:T(8,128)(2,1)S(1)} %shard_map.93), channel_id=1, source_target_pairs={{0,8},{8,0},{16,24},{24,16},{1,9},{9,1},{17,25},{25,17},{2,10},{10... | collective-permute-start | bytes 393224 | tf_op jit(solution)/shard_map/ppermute | solution.py:527
  45.5 0.6 %collective-permute-start.18 = (bf16[512,128]{1,0:T(8,128)(2,1)S(1)}, bf16[512,128]{1,0:T(8,128)(2,1)S(1)}, u32[]{:S(2)}, u32[]{:S(2)}) collective-permute-start(bf16[512,128]{1,0:T(8,128)(2,1)S(1)} %shard_map.94), channel_id=1, source_target_pairs={{0,16},{8,24},{16,0},{24,8},{1,17},{9,25},{17,1},{25,9},{2,18},{10... | collective-permute-start | bytes 393224 | tf_op jit(solution)/shard_map/ppermute | solution.py:526
  46.6 1.4 %shard_map.95 = (bf16[512,128]{1,0:T(8,128)(2,1)S(1)}, bf16[512,128]{1,0:T(8,128)(2,1)S(1)}) custom-call(f32[1]{0:T(128)S(1)} %bitcast.36, f32[512,256]{1,0:T(8,128)S(1)} %get-tuple-element.80.keep_ref, bf16[512,256]{1,0:T(8,128)(2,1)S(1)} %collective-permute-done.9.u_ref, bf16[512,128]{1,0:T(8,128)(2,1)S(1)} %collective-permute-done.14.z_ref, ...), custom_call_target="tpu_custom_call" | custom-call | flops 1000000000 | bytes 3000000 | tf_op jit(solution)/shard_map/pallas_call | solution.py:299
  48.0 1.4 %shard_map.96 = (bf16[512,128]{1,0:T(8,128)(2,1)S(1)}, bf16[512,128]{1,0:T(8,128)(2,1)S(1)}) custom-call(f32[1]{0:T(128)S(1)} %bitcast.38, f32[512,256]{1,0:T(8,128)S(1)} %get-tuple-element.78.keep_ref, bf16[512,256]{1,0:T(8,128)(2,1)S(1)} %collective-permute-done.8.u_ref, bf16[512,128]{1,0:T(8,128)(2,1)S(1)} %collective-permute-done.16.z_ref, ...), custom_call_target="tpu_custom_call" | custom-call | flops 1000000000 | bytes 3000000 | tf_op jit(solution)/shard_map/pallas_call | solution.py:299
  49.5 1.4 %shard_map.97 = (bf16[512,128]{1,0:T(8,128)(2,1)S(1)}, bf16[512,128]{1,0:T(8,128)(2,1)S(1)}) custom-call(f32[1]{0:T(128)S(1)} %bitcast.40, f32[512,256]{1,0:T(8,128)S(1)} %get-tuple-element.86.keep_ref, bf16[512,256]{1,0:T(8,128)(2,1)S(1)} %collective-permute-done.12.u_ref, bf16[512,128]{1,0:T(8,128)(2,1)S(1)} %collective-permute-done.17.z_ref, ...), custom_call_target="tpu_custom_call" | custom-call | flops 1000000000 | bytes 3000000 | tf_op jit(solution)/shard_map/pallas_call | solution.py:299
  50.9 2.2 %shard_map.98 = (bf16[512,512]{1,0:T(8,128)(2,1)}, bf16[512,512]{1,0:T(8,128)(2,1)}) custom-call(f32[1]{0:T(128)S(1)} %bitcast.42, f32[512,256]{1,0:T(8,128)S(1)} %get-tuple-element.88.keep_ref, bf16[512,256]{1,0:T(8,128)(2,1)S(1)} %collective-permute-done.13.u_ref, bf16[512,128]{1,0:T(8,128)(2,1)S(1)} %collective-permute-done.18.z_ref, ...), custom_call_target="tpu_custom_call" | custom-call | flops 1000000000 | bytes 3000000 | tf_op jit(solution)/shard_map/pallas_call | solution.py:299
  (39 shorter events, 3.5 us)
Async XLA Ops:
  0.6 3.8 %copy-start = (bf16[512,2048]{1,0:T(8,128)(2,1)S(1)}, bf16[512,2048]{1,0:T(8,128)(2,1)}, u32[]{:S(2)}) copy-start(bf16[512,2048]{1,0:T(8,128)(2,1)} %x_ref.11) | copy-start | bytes 6291460
  0.6 3.8 %copy-start.1 = (f32[4]{0:T(128)S(1)}, f32[4]{0:T(128)}, u32[]{:S(2)}) copy-start(f32[4]{0:T(128)} %param.11) | copy-start | bytes 52
  0.7 3.8 %copy-start.2 = (bf16[2048,16]{0,1:T(8,128)(2,1)S(1)}, bf16[2048,16]{0,1:T(8,128)(2,1)}, u32[]{:S(2)}) copy-start(bf16[2048,16]{0,1:T(8,128)(2,1)} %param.8) | copy-start | bytes 196612
  0.7 4.6 %collective-permute-start = (bf16[512,2048]{1,0:T(8,128)(2,1)}, bf16[512,2048]{1,0:T(8,128)(2,1)S(1)}, u32[]{:S(2)}, u32[]{:S(2)}) collective-permute-start(bf16[512,2048]{1,0:T(8,128)(2,1)} %x_ref.11), channel_id=1, source_target_pairs={{0,4},{4,0},{1,5},{5,1},{2,6},{6,2},{3,7},{7,3},{8,12},{12,8},{9,1... | collective-permute-start | bytes 6291464 | tf_op jit(solution)/shard_map/ppermute | solution.py:528
  6.0 2.7 %collective-permute-start.1 = (bf16[512,512]{1,0:T(8,128)(2,1)S(1)}, bf16[512,512]{1,0:T(8,128)(2,1)S(1)}, u32[]{:S(2)}, u32[]{:S(2)}) collective-permute-start(bf16[512,512]{1,0:T(8,128)(2,1)S(1)} %shard_map.78), channel_id=1, source_target_pairs={{0,4},{4,0},{1,5},{5,1},{2,6},{6,2},{3,7},{7,3},{8,12},{12,8},{9,1... | collective-permute-start | bytes 1572872 | tf_op jit(solution)/shard_map/ppermute | solution.py:528
  7.2 4.9 %collective-permute-start.2 = (bf16[512,512]{1,0:T(8,128)(2,1)S(1)}, bf16[512,512]{1,0:T(8,128)(2,1)S(1)}, u32[]{:S(2)}, u32[]{:S(2)}) collective-permute-start(bf16[512,512]{1,0:T(8,128)(2,1)S(1)} %shard_map.79), channel_id=1, source_target_pairs={{0,4},{4,0},{1,5},{5,1},{2,6},{6,2},{3,7},{7,3},{8,12},{12,8},{9,1... | collective-permute-start | bytes 1572872 | tf_op jit(solution)/shard_map/ppermute | solution.py:528
  8.2 4.7 %collective-permute-start.3 = (bf16[512,512]{1,0:T(8,128)(2,1)S(1)}, bf16[512,512]{1,0:T(8,128)(2,1)S(1)}, u32[]{:S(2)}, u32[]{:S(2)}) collective-permute-start(bf16[512,512]{1,0:T(8,128)(2,1)S(1)} %shard_map.80), channel_id=1, source_target_pairs={{0,4},{4,0},{1,5},{5,1},{2,6},{6,2},{3,7},{7,3},{8,12},{12,8},{9,1... | collective-permute-start | bytes 1572872 | tf_op jit(solution)/shard_map/ppermute | solution.py:528
  9.4 6.9 %collective-permute-start.4 = (bf16[544,128]{1,0:T(8,128)(2,1)S(1)}, bf16[544,128]{1,0:T(8,128)(2,1)S(1)}, u32[]{:S(2)}, u32[]{:S(2)}) collective-permute-start(bf16[544,128]{1,0:T(8,128)(2,1)S(1)} %get-tuple-element.62), channel_id=1, source_target_pairs={{0,16},{8,24},{16,0},{24,8},{1,17},{9,25},{17,1},{25,9},{2,18},{10... | collective-permute-start | bytes 417800 | tf_op jit(solution)/shard_map/ppermute | solution.py:526
  14.5 11.0 %collective-permute-start.6 = (bf16[512,512]{1,0:T(8,128)(2,1)S(1)}, bf16[512,512]{1,0:T(8,128)(2,1)S(1)}, u32[]{:S(2)}, u32[]{:S(2)}) collective-permute-start(bf16[512,512]{1,0:T(8,128)(2,1)S(1)} %shard_map.84), channel_id=1, source_target_pairs={{0,4},{4,0},{1,5},{5,1},{2,6},{6,2},{3,7},{7,3},{8,12},{12,8},{9,1... | collective-permute-start | bytes 1572872 | tf_op jit(solution)/shard_map/ppermute | solution.py:528
  17.2 9.2 %collective-permute-start.7 = (bf16[512,512]{1,0:T(8,128)(2,1)S(1)}, bf16[512,512]{1,0:T(8,128)(2,1)S(1)}, u32[]{:S(2)}, u32[]{:S(2)}) collective-permute-start(bf16[512,512]{1,0:T(8,128)(2,1)S(1)} %shard_map.86), channel_id=1, source_target_pairs={{0,4},{4,0},{1,5},{5,1},{2,6},{6,2},{3,7},{7,3},{8,12},{12,8},{9,1... | collective-permute-start | bytes 1572872 | tf_op jit(solution)/shard_map/ppermute | solution.py:528
  17.3 6.0 %collective-permute-start.5 = (bf16[512,128]{1,0:T(8,128)(2,1)S(1)}, bf16[512,128]{1,0:T(8,128)(2,1)S(1)}, u32[]{:S(2)}, u32[]{:S(2)}) collective-permute-start(bf16[512,128]{1,0:T(8,128)(2,1)S(1)} %get-tuple-element.72), channel_id=1, source_target_pairs={{0,16},{8,24},{16,0},{24,8},{1,17},{9,25},{17,1},{25,9},{2,18},{10... | collective-permute-start | bytes 393224 | tf_op jit(solution)/shard_map/ppermute | solution.py:526
  19.1 9.2 %collective-permute-start.8 = (bf16[512,256]{1,0:T(8,128)(2,1)S(1)}, bf16[512,256]{1,0:T(8,128)(2,1)S(1)}, u32[]{:S(2)}, u32[]{:S(2)}) collective-permute-start(bf16[512,256]{1,0:T(8,128)(2,1)S(1)} %get-tuple-element.64), channel_id=1, source_target_pairs={{0,8},{8,0},{16,24},{24,16},{1,9},{9,1},{17,25},{25,17},{2,10},{10... | collective-permute-start | bytes 786440 | tf_op jit(solution)/shard_map/ppermute | solution.py:527
  20.6 8.2 %collective-permute-start.9 = (bf16[512,256]{1,0:T(8,128)(2,1)S(1)}, bf16[512,256]{1,0:T(8,128)(2,1)S(1)}, u32[]{:S(2)}, u32[]{:S(2)}) collective-permute-start(bf16[512,256]{1,0:T(8,128)(2,1)S(1)} %get-tuple-element.66), channel_id=1, source_target_pairs={{0,16},{8,24},{16,0},{24,8},{1,17},{9,25},{17,1},{25,9},{2,18},{10... | collective-permute-start | bytes 786440 | tf_op jit(solution)/shard_map/ppermute | solution.py:526
  23.3 9.9 %collective-permute-start.10 = (bf16[544,128]{1,0:T(8,128)(2,1)S(1)}, bf16[544,128]{1,0:T(8,128)(2,1)S(1)}, u32[]{:S(2)}, u32[]{:S(2)}) collective-permute-start(bf16[544,128]{1,0:T(8,128)(2,1)S(1)} %shard_map.85), channel_id=1, source_target_pairs={{0,8},{8,0},{16,24},{24,16},{1,9},{9,1},{17,25},{25,17},{2,10},{10... | collective-permute-start | bytes 417800 | tf_op jit(solution)/shard_map/ppermute | solution.py:527
  25.5 7.7 %collective-permute-start.11 = (bf16[512,128]{1,0:T(8,128)(2,1)S(1)}, bf16[512,128]{1,0:T(8,128)(2,1)S(1)}, u32[]{:S(2)}, u32[]{:S(2)}) collective-permute-start(bf16[512,128]{1,0:T(8,128)(2,1)S(1)} %shard_map.87), channel_id=1, source_target_pairs={{0,8},{8,0},{16,24},{24,16},{1,9},{9,1},{17,25},{25,17},{2,10},{10... | collective-permute-start | bytes 393224 | tf_op jit(solution)/shard_map/ppermute | solution.py:527
  26.3 6.9 %copy-start.3 = (f32[4]{0:T(128)S(1)}, f32[4]{0:T(128)}, u32[]{:S(2)}) copy-start(f32[4]{0:T(128)} %param.9) | copy-start | bytes 52
  26.4 6.9 %copy-start.4 = (f32[4]{0:T(128)S(1)}, f32[4]{0:T(128)}, u32[]{:S(2)}) copy-start(f32[4]{0:T(128)} %param.10) | copy-start | bytes 52
  34.5 12.1 %collective-permute-start.15 = (bf16[768,256]{1,0:T(8,128)(2,1)S(1)}, bf16[768,256]{1,0:T(8,128)(2,1)S(1)}, u32[]{:S(2)}, u32[]{:S(2)}) collective-permute-start(bf16[768,256]{1,0:T(8,128)(2,1)S(1)} %get-tuple-element.84.carry_ref), channel_id=1, source_target_pairs={{0,4},{4,0},{1,5},{5,1},{2,6},{6,2},{3,7},{7,3},{8,12},{12,8},{9,1... | collective-permute-start | bytes 1179656 | tf_op jit(solution)/shard_map/ppermute | solution.py:528
  34.6 9.2 %collective-permute-start.12 = (bf16[512,256]{1,0:T(8,128)(2,1)S(1)}, bf16[512,256]{1,0:T(8,128)(2,1)S(1)}, u32[]{:S(2)}, u32[]{:S(2)}) collective-permute-start(bf16[512,256]{1,0:T(8,128)(2,1)S(1)} %get-tuple-element.76), channel_id=1, source_target_pairs={{0,16},{8,24},{16,0},{24,8},{1,17},{9,25},{17,1},{25,9},{2,18},{10... | collective-permute-start | bytes 786440 | tf_op jit(solution)/shard_map/ppermute | solution.py:526
  34.9 10.5 %collective-permute-start.13 = (bf16[512,256]{1,0:T(8,128)(2,1)S(1)}, bf16[512,256]{1,0:T(8,128)(2,1)S(1)}, u32[]{:S(2)}, u32[]{:S(2)}) collective-permute-start(bf16[512,256]{1,0:T(8,128)(2,1)S(1)} %get-tuple-element.74), channel_id=1, source_target_pairs={{0,8},{8,0},{16,24},{24,16},{1,9},{9,1},{17,25},{25,17},{2,10},{10... | collective-permute-start | bytes 786440 | tf_op jit(solution)/shard_map/ppermute | solution.py:527
  36.6 10.0 %collective-permute-start.14 = (bf16[512,128]{1,0:T(8,128)(2,1)S(1)}, bf16[512,128]{1,0:T(8,128)(2,1)S(1)}, u32[]{:S(2)}, u32[]{:S(2)}) collective-permute-start(bf16[512,128]{1,0:T(8,128)(2,1)S(1)} %shard_map.91), channel_id=1, source_target_pairs={{0,8},{8,0},{16,24},{24,16},{1,9},{9,1},{17,25},{25,17},{2,10},{10... | collective-permute-start | bytes 393224 | tf_op jit(solution)/shard_map/ppermute | solution.py:527
  36.9 11.1 %collective-permute-start.16 = (bf16[512,128]{1,0:T(8,128)(2,1)S(1)}, bf16[512,128]{1,0:T(8,128)(2,1)S(1)}, u32[]{:S(2)}, u32[]{:S(2)}) collective-permute-start(bf16[512,128]{1,0:T(8,128)(2,1)S(1)} %shard_map.90), channel_id=1, source_target_pairs={{0,16},{8,24},{16,0},{24,8},{1,17},{9,25},{17,1},{25,9},{2,18},{10... | collective-permute-start | bytes 393224 | tf_op jit(solution)/shard_map/ppermute | solution.py:526
  43.9 5.6 %collective-permute-start.17 = (bf16[512,128]{1,0:T(8,128)(2,1)S(1)}, bf16[512,128]{1,0:T(8,128)(2,1)S(1)}, u32[]{:S(2)}, u32[]{:S(2)}) collective-permute-start(bf16[512,128]{1,0:T(8,128)(2,1)S(1)} %shard_map.93), channel_id=1, source_target_pairs={{0,8},{8,0},{16,24},{24,16},{1,9},{9,1},{17,25},{25,17},{2,10},{10... | collective-permute-start | bytes 393224 | tf_op jit(solution)/shard_map/ppermute | solution.py:527
  45.5 5.4 %collective-permute-start.18 = (bf16[512,128]{1,0:T(8,128)(2,1)S(1)}, bf16[512,128]{1,0:T(8,128)(2,1)S(1)}, u32[]{:S(2)}, u32[]{:S(2)}) collective-permute-start(bf16[512,128]{1,0:T(8,128)(2,1)S(1)} %shard_map.94), channel_id=1, source_target_pairs={{0,16},{8,24},{16,0},{24,8},{1,17},{9,25},{17,1},{25,9},{2,18},{10... | collective-permute-start | bytes 393224 | tf_op jit(solution)/shard_map/ppermute | solution.py:526
